TPU v7x, 32 devices: a whole 2x2x4 slice. The times are simulated.
32 devices in a mesh: rep: 4 (over x, core), fsdp: 2 (over y), exp: 4 (over z).
Axes of the slice: x: 2, y: 2, z: 4, core: 2. Of those that a mesh axis runs over, the one named last changes fastest.
Arguments:
- tok_grad: bfloat16 [4096, 1440], P(('rep', 'fsdp', 'exp')), may hold values from -18 to 18
- expert_ids: int32 [4096, 4], P(('rep', 'fsdp', 'exp')), may hold values from 0 to 127, all different within a row; in each aligned block of 128 rows (0 to 127, 128 to 255, ...) at most 6 rows name the same one
- route_probs: bfloat16 [4096, 4], P(('rep', 'fsdp', 'exp')), may hold values from 0.049804688 to 1
- hidden_slots: bfloat16 [8, 4, 24, 1440], P(('rep', 'fsdp'), 'exp'), may hold values from -17 to 17
- down_weight: bfloat16 [4, 1440, 1440], P('exp', 'fsdp'), may hold values from -0.15625 to 0.15625
Outputs:
- route_grad: float32 [4096, 4], P(('rep', 'fsdp', 'exp'))
- hidden_grad: bfloat16 [8, 4, 24, 1440], P(('rep', 'fsdp'), 'exp')
- weight_grad: bfloat16 [4, 4, 1440, 1440], P('rep', 'exp', 'fsdp')
Inputs may be any that keep to these rules, and one draw needn't show every extreme that they name: `expert_ids`: each row names 4 different experts. Of one device's rows at most 6 pairs name any one expert, and in every draw some device's rows reach 6 for some expert. Only experts below 4 are handled here.
All inputs are finite; a program needn't handle non-finite values. Where the computation divides by a largest or mean magnitude, that divisor is 1e-20 or more.
Results may differ from a plain program's by a relative error of at most 0.005.
Values may be sent and summed in bfloat16 or wider, within the bound.
No kernel may reach another device: no remote copies, remote signals or barrier semaphores. Data moves between devices by JAX's collectives and lax.ppermute only.
A program may use at most 64 MiB of HBM per device.

v0:
```python
import jax
import jax.numpy as jnp
from jax import lax
from jax.sharding import PartitionSpec as P

clip_level = 40.0


def on_device(tok_grad, expert_ids, route_probs, hidden_slots, down_weight):
    experts = lax.axis_size("exp")
    slot_count = hidden_slots.shape[2]
    capacity = slot_count // experts
    tokens_here = tok_grad.shape[0]
    features = tok_grad.shape[1]
    top_count = expert_ids.shape[1]
    hidden = hidden_slots[0, 0]
    width = hidden.shape[1]
    feature_rows = down_weight.shape[1]
    pairs = expert_ids.reshape(-1)
    expert_iota = jnp.arange(experts, dtype=jnp.int32)
    onehot = (pairs[:, None] == expert_iota[None, :]).astype(jnp.int32)
    before = jnp.cumsum(onehot, axis=0, dtype=jnp.int32) - onehot
    order = jnp.sum(before * onehot, axis=1, dtype=jnp.int32)
    target = jnp.where(pairs < experts, pairs * capacity + order, -1).reshape(
        tokens_here, top_count
    )
    slot_iota = jnp.arange(slot_count, dtype=jnp.int32)
    matches = target[None, :, :] == slot_iota[:, None, None]
    picker = jnp.any(matches, axis=2).astype(jnp.bfloat16)
    send_rows = jnp.dot(picker, tok_grad, preferred_element_type=jnp.float32).astype(jnp.bfloat16)
    send_rows = send_rows.reshape(experts, capacity, features)
    send_probs = jnp.sum(
        jnp.where(matches, route_probs.astype(jnp.float32)[None, :, :], 0.0), axis=(1, 2)
    )
    send_probs = send_probs.astype(jnp.bfloat16).reshape(experts, capacity)
    got_rows, got_probs = (
        lax.all_to_all(send_rows, "exp", split_axis=0, concat_axis=0, tiled=True),
        lax.all_to_all(send_probs, "exp", split_axis=0, concat_axis=0, tiled=True),
    )
    got_rows = got_rows.reshape(slot_count, features)
    got_probs = got_probs.reshape(slot_count)
    scaled = (got_probs.astype(jnp.float32)[:, None] * got_rows.astype(jnp.float32)).astype(
        jnp.bfloat16
    )
    block = lax.all_gather(down_weight, "fsdp", axis=1, tiled=True)[0]
    outputs = lax.dot_general(
        hidden, block, (((1,), (1,)), ((), ())), preferred_element_type=jnp.float32
    )
    score_acc = jnp.sum(got_rows.astype(jnp.float32) * outputs, axis=1)
    hidden_acc = jnp.dot(scaled, block, preferred_element_type=jnp.float32)
    hidden_acc, score_acc = (hidden_acc, score_acc)
    hidden_grad = hidden_acc.astype(jnp.bfloat16).reshape(1, 1, slot_count, width)
    returned = lax.all_to_all(
        score_acc.reshape(experts, capacity), "exp", split_axis=0, concat_axis=0, tiled=True
    )
    returned = returned.reshape(slot_count)
    route_grad = jnp.sum(jnp.where(matches, returned[:, None, None], 0.0), axis=0)
    group_hidden = lax.all_gather(hidden, "fsdp", axis=0, tiled=True)
    group_scaled = lax.all_to_all(scaled, "fsdp", split_axis=1, concat_axis=0, tiled=True)
    summed = lax.dot_general(
        group_scaled, group_hidden, (((0,), (0,)), ((), ())), preferred_element_type=jnp.float32
    )
    local_peak = jnp.max(jnp.abs(summed))
    peak = lax.pmax(local_peak, ("rep", "fsdp"))
    factor = jnp.minimum(1.0, clip_level / (peak + 1e-06))
    weight_grad = (summed * factor).astype(jnp.bfloat16).reshape(1, 1, feature_rows, width)
    return (route_grad, hidden_grad, weight_grad)


def solution(mesh):
    placed = (
        P(("rep", "fsdp", "exp"), None),
        P(("rep", "fsdp", "exp"), None),
        P(("rep", "fsdp", "exp"), None),
        P(("rep", "fsdp"), "exp", None, None),
        P("exp", "fsdp", None),
    )
    return jax.shard_map(
        on_device,
        mesh=mesh,
        in_specs=placed,
        out_specs=(
            P(("rep", "fsdp", "exp"), None),
            P(("rep", "fsdp"), "exp", None, None),
            P("rep", "exp", "fsdp", None),
        ),
        check_vma=False,
    )
```

profile of v0, /device:TPU:0, one launch (start us, length us, event | category | flops | bytes accessed | tf_op | source)
XLA Modules:
  0.0 135.3 jit_solution(12972022279385396969)
XLA Ops:
  7.2 0.7 all-gather.3.cloned.1.call-update
  7.9 0.8 copy.38
  8.8 0.1 eq.38
  8.9 1.2 reduce-window.6
  10.2 0.2 slice_reduce_fusion
  10.4 0.2 reduce-window.9
  10.7 0.1 reduce_sum.39
  10.8 0.7 add_select_fusion
  11.6 0.2 convolution_convert_fusion
  11.8 0.7 reshape.96
  12.5 6.3 %all-to-all-start = ((bf16[4,6,1440]{2,1,0:T(8,128)(2,1)}), bf16[4,6,1440]{2,1,0:T(8,128)(2,1)S(1)}, u32[]{:S(2)}, u32[]{:S(2)}) async-start(bf16[4,6,1440]{2,1,0:T(8,128)(2,1)} %reshape.96), calls=%async_computation | async-start | bytes 196608 | tf_op jit(solution)/shard_map/all_to_all | solution.py:37
  18.8 5.6 %all-gather = bf16[1,1,48,1440]{3,2,1,0:T(8,128)(2,1)S(1)} all-gather(bf16[1,1,24,1440]{3,2,1,0:T(8,128)(2,1)} %param.8), channel_id=2, replica_groups=mesh['rep'=4,'fsdp'=2,'exp'=4] {'fsdp'}, dimensions={2}, use_global_device_ids=true | all-gather | bytes 207360 | tf_op jit(solution)/shard_map/all_gather | solution.py:58
  24.4 0.2 all-to-all-done
  24.7 47.0 %all-gather.3.cloned.1.call-done = bf16[1,1440,1440]{2,1,0:T(8,128)(2,1)} async-done(((bf16[1,720,1440]{2,1,0:T(8,128)(2,1)}), bf16[1,1440,1440]{2,1,0:T(8,128)(2,1)}) %all-gather.3.cloned.1.call-update) | async-done | bytes 4147216 | tf_op jit(solution)/shard_map/all_gather | solution.py:45
  71.7 3.7 %fusion.14 = f32[24]{0:T(128)S(1)} fusion(f32[24,1440]{1,0:T(8,128)S(1)} %reshape.99, bf16[1,1440,1440]{2,1,0:T(8,128)(2,1)} %all-gather.3.cloned.1.call-done, bf16[1,1,24,1440]{3,2,1,0:T(8,128)(2,1)} %param.8), kind=kOutput, calls=%fused_computation.11 | convolution fusion | flops 99601896 | bytes 4354656 | tf_op jit(solution)/shard_map/dot_general | solution.py:46
  75.4 0.7 all_to_all.26
  76.1 5.1 %all-to-all-start.1 = ((f32[4,1,6]{2,1,0:T(1,128)}), f32[4,1,6]{2,1,0:T(1,128)S(1)}, u32[]{:S(2)}, u32[]{:S(2)}) async-start(f32[4,1,6]{2,1,0:T(1,128)} %bitcast.3), calls=%async_computation.1 | async-start | bytes 4096 | tf_op jit(solution)/shard_map/all_to_all | solution.py:53
  81.2 5.5 %all-to-all-done.1 = f32[4,1,6]{2,1,0:T(1,128)S(1)} async-done(((f32[4,1,6]{2,1,0:T(1,128)}), f32[4,1,6]{2,1,0:T(1,128)S(1)}, u32[]{:S(2)}, u32[]{:S(2)}) %all-to-all-start.1) | async-done | bytes 128 | tf_op jit(solution)/shard_map/all_to_all | solution.py:53
  86.6 0.5 broadcast.39
  87.2 0.7 reduce.9
  87.9 0.7 select_reduce_fusion
  88.6 0.7 convert_element_type.99
  89.2 3.2 %all-to-all-start.2 = ((bf16[4,1,6]{2,1,0:T(2,128)(2,1)}), bf16[4,1,6]{2,1,0:T(2,128)(2,1)S(1)}, u32[]{:S(2)}, u32[]{:S(2)}) async-start(bf16[4,1,6]{2,1,0:T(2,128)(2,1)} %convert_element_type.99), calls=%async_computation.2 | async-start | bytes 4096 | tf_op jit(solution)/shard_map/all_to_all | solution.py:38
  92.5 0.2 reshape.102
  92.7 5.3 %all-to-all-done.2 = bf16[4,1,6]{2,1,0:T(2,128)(2,1)S(1)} async-done(((bf16[4,1,6]{2,1,0:T(2,128)(2,1)}), bf16[4,1,6]{2,1,0:T(2,128)(2,1)S(1)}, u32[]{:S(2)}, u32[]{:S(2)}) %all-to-all-start.2) | async-done | bytes 80 | tf_op jit(solution)/shard_map/all_to_all | solution.py:38
  98.2 0.7 fusion.19
  98.9 3.3 %all-to-all-start.3 = ((bf16[24,2,720]{2,0,1:T(8,128)(2,1)}), bf16[24,2,720]{2,0,1:T(8,128)(2,1)S(1)}, u32[]{:S(2)}, u32[]{:S(2)}) async-start(bf16[24,2,720]{2,0,1:T(8,128)(2,1)} %fusion.19), calls=%async_computation.3 | async-start | bytes 147456 | tf_op jit(solution)/shard_map/all_to_all | solution.py:59
  102.2 3.6 %fusion.10 = bf16[1,1,24,1440]{3,2,1,0:T(8,128)(2,1)} fusion(bf16[24,1440]{1,0:T(8,128)(2,1)S(1)} %convert_element_type.87, bf16[1,1440,1440]{2,1,0:T(8,128)(2,1)} %all-gather.3.cloned.1.call-done), kind=kOutput, calls=%fused_computation.9 | convolution fusion | flops 99567360 | bytes 4285440 | tf_op jit(solution)/shard_map/dot_general | solution.py:50
  105.8 0.6 all-to-all-done.3
  106.4 3.4 %abs_reduce_fusion = (f32[]{:T(128)}, f32[720,1440]{1,0:T(8,128)}) fusion(bf16[48,720]{1,0:T(8,128)(2,1)S(1)} %bitcast.53, bf16[1,1,48,1440]{3,2,1,0:T(8,128)(2,1)S(1)} %all-gather), kind=kOutput, calls=%fused_computation.5 | convolution fusion | flops 101606400 | bytes 4354564 | tf_op jit(solution)/shard_map/dot_general | solution.py:60
  109.7 14.0 %pmax.7 = f32[]{:T(128)} all-reduce(f32[]{:T(128)} %get-tuple-element.5), channel_id=1, replica_groups=mesh['rep'=4,'fsdp'=2,'exp'=4] {'rep','fsdp'}, use_global_device_ids=true, to_apply=%region_8.9 | all-reduce | flops 1 | bytes 8 | tf_op jit(solution)/shard_map/pmax | solution.py:64
  124.4 4.1 %fusion.13 = bf16[1,1,720,1440]{3,2,1,0:T(8,128)(2,1)} fusion(f32[720,1440]{1,0:T(8,128)} %get-tuple-element.6, f32[]{:T(128)S(6)} %min_shard_map.3), kind=kLoop, calls=%fused_computation.10 | loop fusion | flops 2073600 | bytes 6220804 | tf_op jit(solution)/shard_map/reshape | solution.py:66
  (19 shorter events, 0.7 us)
Async XLA Ops:
  7.2 4.4 %copy-start = (bf16[128,1440]{0,1:T(8,128)(2,1)S(1)}, bf16[128,1440]{0,1:T(8,128)(2,1)}, u32[]{:S(2)}) copy-start(bf16[128,1440]{0,1:T(8,128)(2,1)} %param.5) | copy-start | bytes 1105924
  7.2 74.0 %copy-start.1 = (bf16[128,4]{0,1:T(4,128)(2,1)S(1)}, bf16[128,4]{0,1:T(4,128)(2,1)}, u32[]{:S(2)}) copy-start(bf16[128,4]{0,1:T(4,128)(2,1)} %param.7) | copy-start | bytes 3076
  7.2 64.5 %all-gather.3.cloned.1.call-start = ((), (), s32[]{:S(2)}) async-start(), calls=%async_computation.4 | async-start | bytes 6635520 | tf_op jit(solution)/shard_map/all_gather | solution.py:45
  12.5 12.2 %all-to-all-start = ((bf16[4,6,1440]{2,1,0:T(8,128)(2,1)}), bf16[4,6,1440]{2,1,0:T(8,128)(2,1)S(1)}, u32[]{:S(2)}, u32[]{:S(2)}) async-start(bf16[4,6,1440]{2,1,0:T(8,128)(2,1)} %reshape.96), calls=%async_computation | async-start | bytes 196608 | tf_op jit(solution)/shard_map/all_to_all | solution.py:37
  76.1 10.6 %all-to-all-start.1 = ((f32[4,1,6]{2,1,0:T(1,128)}), f32[4,1,6]{2,1,0:T(1,128)S(1)}, u32[]{:S(2)}, u32[]{:S(2)}) async-start(f32[4,1,6]{2,1,0:T(1,128)} %bitcast.3), calls=%async_computation.1 | async-start | bytes 4096 | tf_op jit(solution)/shard_map/all_to_all | solution.py:53
  89.2 8.7 %all-to-all-start.2 = ((bf16[4,1,6]{2,1,0:T(2,128)(2,1)}), bf16[4,1,6]{2,1,0:T(2,128)(2,1)S(1)}, u32[]{:S(2)}, u32[]{:S(2)}) async-start(bf16[4,1,6]{2,1,0:T(2,128)(2,1)} %convert_element_type.99), calls=%async_computation.2 | async-start | bytes 4096 | tf_op jit(solution)/shard_map/all_to_all | solution.py:38
  98.9 7.5 %all-to-all-start.3 = ((bf16[24,2,720]{2,0,1:T(8,128)(2,1)}), bf16[24,2,720]{2,0,1:T(8,128)(2,1)S(1)}, u32[]{:S(2)}, u32[]{:S(2)}) async-start(bf16[24,2,720]{2,0,1:T(8,128)(2,1)} %fusion.19), calls=%async_computation.3 | async-start | bytes 147456 | tf_op jit(solution)/shard_map/all_to_all | solution.py:59
Sparse Core Ops, SparseCore 0:
  9.5 62.1 all-gather.2
where the time goes:
time: 136 us; the launch traced here: 135 us
  waiting for transfers between devices  59.2 us (44%)
  blocking collectives  19.6 us (14%)
  starting transfers between devices  18 us (13%)
  between operations  14.8 us (11%)
  matrix products  10.8 us (8%)
  other arithmetic  8.5 us (6%)
  local copies, waits for them, and re-layouts  4.37 us (3%)
    all_gather x1, waiting for transfers between devices, on_device(): block = lax.all_gather(down_weight, 'fsdp', axis=1, tiled=True)[0]  47 us
    pmax x1, blocking collectives, on_device(): peak = lax.pmax(local_peak, ('rep', 'fsdp'))  14 us
    all_to_all x1, starting transfers between devices, on_device(): lax.all_to_all(send_rows, 'exp', split_axis=0, concat_axis=0, tiled=True)  6.35 us
    all_gather x1, blocking collectives, on_device(): group_hidden = lax.all_gather(hidden, 'fsdp', axis=0, tiled=True)  5.6 us
    all_to_all x1, waiting for transfers between devices, on_device(): lax.all_to_all(score_acc.reshape(experts, capacity), 'exp', split_axis=0,...  5.49 us
    all_to_all x1, waiting for transfers between devices, on_device(): lax.all_to_all(send_probs, 'exp', split_axis=0, concat_axis=0, tiled=True)  5.28 us
    all_to_all x1, starting transfers between devices, on_device(): lax.all_to_all(score_acc.reshape(experts, capacity), 'exp', split_axis=0,...  5.09 us
    reshape x1, other arithmetic, on_device(): (summed * factor).astype(jnp.bfloat16).reshape(1, 1, feature_rows, width)  4.11 us
  transfers between devices with their start and end apart: 5, of which 5 were waited for; matrix products, arithmetic and copies ran while one was open for 6% of the time, Pallas kernels for 0%

commit v1 on v0

v1 whole, which is shorter than its diff:
```python
import functools

import jax
import jax.numpy as jnp
from jax import lax
from jax.experimental import pallas as pl
from jax.experimental.pallas import tpu as pltpu
from jax.sharding import PartitionSpec as P

clip_level = 40.0
f32 = jnp.float32
bf16 = jnp.bfloat16
VMEM = pltpu.VMEM


def round_up(n, m):
    return (n + m - 1) // m * m


def iota(shape, dim):
    return lax.broadcasted_iota(jnp.int32, shape, dim)


def dot(a, b, dims):
    return lax.dot_general(a, b, (dims, ((), ())), preferred_element_type=f32)


def call(kernel, outs, flops, name, scratch=(), out_specs=None, in_specs=None):
    def run(*args):
        specs = in_specs or [pl.BlockSpec(memory_space=VMEM)] * len(args)
        return pl.pallas_call(
            kernel,
            out_shape=outs,
            in_specs=specs,
            out_specs=out_specs or [pl.BlockSpec(memory_space=VMEM)] * len(outs),
            scratch_shapes=list(scratch),
            compiler_params=pltpu.CompilerParams(vmem_limit_bytes=48 * 1024 * 1024),
            cost_estimate=pl.CostEstimate(flops=flops, bytes_accessed=1 << 20, transcendentals=0),
            name=name,
        )(*args)

    return run


def route_kernel(fsdp, room, ids_ref, probs_ref, tok_ref, send_ref, taken_ref):
    choices, tokens = ids_ref.shape
    slots = taken_ref.shape[0]
    part = tok_ref.shape[0] // fsdp
    width = send_ref.shape[2]
    slot = iota((slots, tokens), 0)
    expert = slot // room
    named = jnp.zeros((slots, tokens), jnp.bool_)
    prob = jnp.zeros((slots, tokens), f32)
    for k in range(choices):
        hit = ids_ref[k : k + 1, :] == expert
        named = named | hit
        prob = jnp.where(hit, probs_ref[k : k + 1, :].astype(f32), prob)
    earlier = (iota((tokens, tokens), 0) < iota((tokens, tokens), 1)).astype(bf16)
    order = dot(jnp.where(named, 1.0, 0.0).astype(bf16), earlier, ((1,), (0,)))
    taken = named & (order == (slot - expert * room).astype(f32))
    picker = jnp.where(taken, 1.0, 0.0)
    taken_ref[...] = picker
    prob = jnp.sum(jnp.where(taken, prob, 0.0), axis=1, keepdims=True)
    lane = iota((slots, width - part), 1)
    tail = jnp.where(lane == 0, prob, 0.0).astype(bf16)
    picker = picker.astype(bf16)
    for f in range(fsdp):
        rows = dot(picker, tok_ref[f * part : (f + 1) * part, :], ((1,), (1,))).astype(bf16)
        block = jnp.concatenate([rows, tail], axis=1)
        count = slots // room
        send_ref[f * count : (f + 1) * count] = block.reshape(count, room, width)


def outputs_kernel(capacity, room, *refs):
    hidden_refs, weight_ref, padded_ref, outputs_ref = refs[:-3], refs[-3], refs[-2], refs[-1]
    fsdp = len(hidden_refs)
    rows = padded_ref.shape[0] // fsdp
    slot_count = hidden_refs[0].shape[0]
    me = lax.axis_index("fsdp")
    to, at = iota((rows, slot_count), 0), iota((rows, slot_count), 1)
    source, order = to // room, to % room
    spread = jnp.where((order < capacity) & (at == source * capacity + order), 1.0, 0.0).astype(bf16)
    for d, ref in enumerate(hidden_refs):
        group = lax.rem(me + fsdp - d, fsdp)
        where = pl.ds(pl.multiple_of(group * rows, rows), rows)
        padded_ref[where, :] = dot(spread, ref[...], ((1,), (0,))).astype(bf16)
    outputs_ref[...] = dot(padded_ref[...], weight_ref[...], ((1,), (1,)))


def summed_kernel(replicas, got_ref, padded_ref, outputs_ref, summed_ref, scaled_ref, pack_ref):
    blocks, room, width = got_ref.shape
    total = blocks * room
    part = outputs_ref.shape[1]
    got = got_ref[...].reshape(total, width)
    rows = got[:, :part].astype(f32)
    prob = got[:, part : part + 1].astype(f32)
    scaled = (prob * rows).astype(bf16)
    scaled_ref[...] = scaled
    summed = dot(scaled, padded_ref[...], ((0,), (0,)))
    summed_ref[...] = summed
    peak = jnp.max(jnp.abs(summed))
    score = jnp.sum(rows * outputs_ref[...], axis=1, keepdims=True)
    lane = iota((total, 128), 1)
    order = iota((total, 128), 0) % room
    spread = jnp.where(lane == order, score, 0.0).reshape(blocks, room, 128)
    packed = jnp.sum(spread, axis=1)
    packed = jnp.where(iota((blocks, 128), 1) == room, peak, packed)
    for r in range(replicas):
        pack_ref[r * blocks : (r + 1) * blocks, 0, :] = packed


def hidden_kernel(capacity, room, scaled_ref, weight_ref, own_ref, *send_refs):
    fsdp = len(send_refs) + 1
    total = scaled_ref.shape[0]
    rows = total // fsdp
    slot_count = own_ref.shape[0]
    me = lax.axis_index("fsdp")
    to, at = iota((slot_count, rows), 0), iota((slot_count, rows), 1)
    pick = jnp.where(at == to // capacity * room + to % capacity, 1.0, 0.0).astype(bf16)
    for d, ref in enumerate((own_ref,) + send_refs):
        group = lax.rem(me + d, fsdp)
        where = pl.ds(pl.multiple_of(group * rows, rows), rows)
        dense = dot(pick, scaled_ref[where, :], ((1,), (0,))).astype(bf16)
        ref[...] = dot(dense, weight_ref[...], ((1,), (0,))).astype(ref.dtype)


def final_kernel(
    experts, fsdp, room, recv_ref, summed_ref, ids_ref, taken_ref, weight_ref, route_ref, held, sems
):
    devices = recv_ref.shape[0]
    blocks = fsdp * experts
    replica, expert = lax.axis_index("rep"), lax.axis_index("exp")
    recv = recv_ref[...].reshape(devices, 128)
    row, lane = iota((devices, 128), 0), iota((devices, 128), 1)
    peak = jnp.max(jnp.where((lane == room) & (row % experts == expert), recv, 0.0))
    factor = jnp.minimum(1.0, clip_level / (jnp.full((1, 1), peak, f32) + 1e-06))
    chunks = sems.shape[0]
    size = summed_ref.shape[0] // chunks
    copies = []
    for c in range(chunks):
        part = slice(c * size, (c + 1) * size)
        held[part, :] = (summed_ref[part, :] * factor).astype(bf16)
        copy = pltpu.make_async_copy(held.at[part, :], weight_ref.at[part, :], sems.at[c])
        copy.start()
        copies.append(copy)
    slots, tokens = taken_ref.shape
    mine = jnp.zeros((experts, 128), f32)
    for f in range(fsdp):
        start = replica * blocks + f * experts
        mine = mine + recv_ref[pl.ds(start, experts), 0, :]
    spread = jnp.broadcast_to(mine[:, None, :], (experts, room, 128)).reshape(slots, 128)
    order = iota((slots, 128), 0) % room
    score = jnp.sum(jnp.where(iota((slots, 128), 1) == order, spread, 0.0), axis=1, keepdims=True)
    slot_expert = iota((slots, tokens), 0) // room
    found = taken_ref[...] * score
    for k in range(ids_ref.shape[0]):
        hit = ids_ref[k : k + 1, :] == slot_expert
        route_ref[k : k + 1, :] = jnp.sum(jnp.where(hit, found, 0.0), axis=0, keepdims=True)
    for copy in copies:
        copy.wait()


def on_device(tok_grad, expert_ids, route_probs, hidden_slots, down_weight):
    experts, fsdp, replicas = lax.axis_size("exp"), lax.axis_size("fsdp"), lax.axis_size("rep")
    slot_count, width = hidden_slots.shape[2:]
    capacity = slot_count // experts
    room = round_up(capacity, 8)
    tokens, features = tok_grad.shape
    choices = expert_ids.shape[1]
    part = down_weight.shape[1]
    padded = round_up(part + 1, 128)
    blocks, slots = fsdp * experts, experts * room
    total = blocks * room
    devices = replicas * blocks
    shape = jax.ShapeDtypeStruct
    hidden, weight = hidden_slots[0, 0], down_weight[0]
    ids = expert_ids.T

    def ring(d):
        return [(i, (i + d) % fsdp) for i in range(fsdp)]

    send, taken = call(
        functools.partial(route_kernel, fsdp, room),
        [shape((blocks, room, padded), bf16), shape((slots, tokens), f32)],
        2 * slots * tokens * features,
        "route",
    )(ids, route_probs.T, tok_grad.T)
    got = lax.all_to_all(send, ("fsdp", "exp"), split_axis=0, concat_axis=0, tiled=True)
    hiddens = [hidden] + [lax.ppermute(hidden, "fsdp", ring(d)) for d in range(1, fsdp)]
    hidden_padded, outputs = call(
        functools.partial(outputs_kernel, capacity, room),
        [shape((total, width), bf16), shape((total, part), f32)],
        2 * total * part * width,
        "outputs",
    )(*hiddens, weight)
    summed, scaled, pack = call(
        functools.partial(summed_kernel, replicas),
        [shape((part, width), f32), shape((total, part), bf16), shape((devices, 1, 128), f32)],
        2 * total * part * width,
        "summed",
    )(got, hidden_padded, outputs)
    recv = lax.all_to_all(pack, ("rep", "fsdp", "exp"), split_axis=0, concat_axis=0, tiled=True)
    own, *others = call(
        functools.partial(hidden_kernel, capacity, room),
        [shape((slot_count, width), f32)] + [shape((slot_count, width), bf16)] * (fsdp - 1),
        2 * total * part * width,
        "hidden",
    )(scaled, weight)
    hidden_acc = own
    for d in range(1, fsdp):
        hidden_acc = hidden_acc + lax.ppermute(others[d - 1], "fsdp", ring(d)).astype(f32)
    hidden_grad = hidden_acc.astype(bf16).reshape(1, 1, slot_count, width)
    sizes = [c for c in range(16, 161, 16) if part % c == 0] or [part]
    chunks = part // sizes[-1]
    weight_grad, route_grad = call(
        functools.partial(final_kernel, experts, fsdp, room),
        [shape((part, width), bf16), shape((choices, tokens), f32)],
        part * width,
        "final",
        scratch=[VMEM((part, width), bf16), pltpu.SemaphoreType.DMA((chunks,))],
        out_specs=[pl.BlockSpec(memory_space=pl.ANY), pl.BlockSpec(memory_space=VMEM)],
    )(recv, summed, ids, taken)
    return route_grad.T, hidden_grad, weight_grad.reshape(1, 1, part, width)


def solution(mesh):
    placed = (
        P(("rep", "fsdp", "exp"), None),
        P(("rep", "fsdp", "exp"), None),
        P(("rep", "fsdp", "exp"), None),
        P(("rep", "fsdp"), "exp", None, None),
        P("exp", "fsdp", None),
    )
    return jax.shard_map(
        on_device,
        mesh=mesh,
        in_specs=placed,
        out_specs=(
            P(("rep", "fsdp", "exp"), None),
            P(("rep", "fsdp"), "exp", None, None),
            P("rep", "exp", "fsdp", None),
        ),
        check_vma=False,
    )
```

time: 136 us -> 38.2 us (0.28)
  waiting for transfers between devices: 59.2 us -> 2.94 us
  between operations: 14.8 us -> 0.69 us
  matrix products: 10.8 us -> 0 us
  blocking collectives: 19.6 us -> 11.4 us
  other arithmetic: 8.5 us -> 0.65 us
  starting transfers between devices: 18 us -> 11.1 us
  Pallas kernels: 0 us -> 6.17 us
    all_gather x1 -> x0, waiting for transfers between devices: 47 us -> none  [on_device(): block = lax.all_gather(down_weight, 'fsdp', axis=1, tiled=True)[0]]
    pmax x1 -> x0, blocking collectives: 14 us -> none  [on_device(): peak = lax.pmax(local_peak, ('rep', 'fsdp'))]
    all_to_all x4 -> x1, waiting for transfers between devices: 11.6 us -> 0.01 us  [on_device(): lax.all_to_all(send, ('fsdp', 'exp'), split_axis=0, concat_axis=0, tiled=...]
    all_to_all x0 -> x1, blocking collectives: none -> 11.4 us  [on_device(): lax.all_to_all(pack, ('rep', 'fsdp', 'exp'), split_axis=0, concat_axis=0,...]
    dot_general x4 -> x0, matrix products: 10.8 us -> none  [the longest x1 3.67 us: on_device(): lax.dot_general(hidden, block, (((1,), (1,)), ((), ())), preferred_elemen...]
    all_to_all x4 -> x1, starting transfers between devices: 18 us -> 7.31 us  [on_device(): lax.all_to_all(send, ('fsdp', 'exp'), split_axis=0, concat_axis=0, tiled=...]
    pallas_call x0 -> x5, Pallas kernels: none -> 6.17 us  [run(): pl.pallas_call(kernel, out_shape=outs, in_specs=specs, out_specs=out_spec...]
    all_gather x1 -> x0, blocking collectives: 5.6 us -> none  [on_device(): group_hidden = lax.all_gather(hidden, 'fsdp', axis=0, tiled=True)]
  transfers between devices with their start and end apart: 5 -> 3, of which waited for: 5 -> 1; matrix products, arithmetic and copies ran while one was open for 6% -> 0% of each run, Pallas kernels for 0% -> 8%
where the time goes in v1:
time: 38.2 us; the launch traced here: 37.9 us
  blocking collectives  11.4 us (30%)
  starting transfers between devices  11.1 us (29%)
  Pallas kernels  6.17 us (16%)
  local copies, waits for them, and re-layouts  4.85 us (13%)
  waiting for transfers between devices  2.94 us (8%)
  between operations  0.69 us (2%)
  other arithmetic  0.65 us (2%)
    all_to_all x1, blocking collectives, on_device(): lax.all_to_all(pack, ('rep', 'fsdp', 'exp'), split_axis=0, concat_axis=0,...  11.4 us
    all_to_all x1, starting transfers between devices, on_device(): lax.all_to_all(send, ('fsdp', 'exp'), split_axis=0, concat_axis=0, tiled=...  7.31 us
    pallas_call x5, Pallas kernels, run(): pl.pallas_call(kernel, out_shape=outs, in_specs=specs, out_specs=out_spec...  6.17 us
    unnamed x14, local copies, waits for them, and re-layouts  4.85 us
    ppermute x1, waiting for transfers between devices, on_device(): lax.ppermute(hidden, 'fsdp', ring(d))  2.93 us
    ppermute x1, starting transfers between devices, on_device(): lax.ppermute(hidden, 'fsdp', ring(d))  2.02 us
    ppermute x1, starting transfers between devices, on_device(): lax.ppermute(others[d - 1], 'fsdp', ring(d)).astype(f32)  1.77 us
  transfers between devices with their start and end apart: 3, of which 1 were waited for; matrix products, arithmetic and copies ran while one was open for 0% of the time, Pallas kernels for 8%

profile of v1, /device:TPU:0, one launch (start us, length us, event | category | flops | bytes accessed | tf_op | source)
XLA Modules:
  0.0 37.9 jit_solution(15721502153250662988)
XLA Ops:
  0.6 0.0 copy-start.2
  0.6 1.0 %copy-done.2 = bf16[128,1440]{0,1:T(8,128)(2,1)S(1)} copy-done((bf16[128,1440]{0,1:T(8,128)(2,1)S(1)}, bf16[128,1440]{0,1:T(8,128)(2,1)}, u32[]{:S(2)}) %copy-start.2) | copy-done | bytes 368664
  1.6 0.0 copy-start.4
  1.6 0.7 %copy-done.4 = s32[128,4]{0,1:T(4,128)S(1)} copy-done((s32[128,4]{0,1:T(4,128)S(1)}, s32[128,4]{0,1:T(4,128)}, u32[]{:S(2)}) %copy-start.4) | copy-done | bytes 2072
  2.3 0.0 copy-start.6
  2.3 0.7 %copy-done.6 = bf16[128,4]{0,1:T(4,128)(2,1)S(1)} copy-done((bf16[128,4]{0,1:T(4,128)(2,1)S(1)}, bf16[128,4]{0,1:T(4,128)(2,1)}, u32[]{:S(2)}) %copy-start.6) | copy-done | bytes 1048
  3.0 1.0 %route.1 = (bf16[8,8,768]{2,1,0:T(8,128)(2,1)}, f32[32,128]{1,0:T(8,128)S(1)}) custom-call(s32[4,128]{1,0:T(4,128)S(1)} %bitcast.14, bf16[4,128]{1,0:T(4,128)(2,1)S(1)} %bitcast.16, bf16[1440,128]{1,0:T(8,128)(2,1)S(1)} %bitcast.11), custom_call_target="tpu_custom_call" | custom-call | flops 11796480 | bytes 1048576 | tf_op jit(solution)/shard_map/route/pallas_call | solution.py:31
  4.0 7.3 %all-to-all-start = ((bf16[8,8,768]{2,1,0:T(8,128)(2,1)}), bf16[8,8,768]{2,1,0:T(8,128)(2,1)S(1)}, u32[]{:S(2)}, u32[]{:S(2)}) async-start(bf16[8,8,768]{2,1,0:T(8,128)(2,1)} %get-tuple-element.14), calls=%async_computation | async-start | bytes 196608 | tf_op jit(solution)/shard_map/all_to_all | solution.py:188
  11.3 2.0 %collective-permute-start = (bf16[24,1440]{1,0:T(8,128)(2,1)}, bf16[24,1440]{1,0:T(8,128)(2,1)S(1)}, u32[]{:S(2)}, u32[]{:S(2)}) collective-permute-start(bf16[24,1440]{1,0:T(8,128)(2,1)} %bitcast.12), channel_id=1, source_target_pairs={{0,4},{4,0},{1,5},{5,1},{2,6},{6,2},{3,7},{7,3},{8,12},{12,8},{9,1... | collective-permute-start | bytes 207368 | tf_op jit(solution)/shard_map/ppermute | solution.py:189
  13.3 2.9 %collective-permute-done.refs_1_ = bf16[24,1440]{1,0:T(8,128)(2,1)S(1)} collective-permute-done((bf16[24,1440]{1,0:T(8,128)(2,1)}, bf16[24,1440]{1,0:T(8,128)(2,1)S(1)}, u32[]{:S(2)}, u32[]{:S(2)}) %collective-permute-start) | collective-permute-done | bytes 69152 | tf_op jit(solution)/shard_map/ppermute | solution.py:189
  16.3 0.0 copy-start
  16.3 1.6 %copy-done = bf16[1,720,1440]{2,1,0:T(8,128)(2,1)S(1)} copy-done((bf16[1,720,1440]{2,1,0:T(8,128)(2,1)S(1)}, bf16[1,720,1440]{2,1,0:T(8,128)(2,1)}, u32[]{:S(2)}) %copy-start) | copy-done | bytes 2073624
  17.9 0.0 copy-start.3
  17.9 0.9 %copy-done.3 = bf16[1,1,24,1440]{3,2,1,0:T(8,128)(2,1)S(1)} copy-done((bf16[1,1,24,1440]{3,2,1,0:T(8,128)(2,1)S(1)}, bf16[1,1,24,1440]{3,2,1,0:T(8,128)(2,1)}, u32[]{:S(2)}) %copy-start.3) | copy-done | bytes 69144
  18.8 0.0 copy-start.1
  18.8 0.0 copy-start.5
  18.8 0.9 %outputs.1 = (bf16[64,1440]{1,0:T(8,128)(2,1)S(1)}, f32[64,720]{1,0:T(8,128)S(1)}) custom-call(bf16[24,1440]{1,0:T(8,128)(2,1)S(1)} %bitcast.13, bf16[24,1440]{1,0:T(8,128)(2,1)S(1)} %collective-permute-done.refs_1_, bf16[720,1440]{1,0:T(8,128)(2,1)S(1)} %bitcast.9), custom_call_target="tpu_custom_call" | custom-call | flops 132710400 | bytes 1048576 | tf_op jit(solution)/shard_map/outputs/pallas_call | solution.py:31
  19.7 0.0 all-to-all-done.got_ref
  19.7 1.0 %summed.1 = (f32[720,1440]{1,0:T(8,128)S(1)}, bf16[64,720]{1,0:T(8,128)(2,1)S(1)}, f32[32,1,128]{2,1,0:T(1,128)S(1)}) custom-call(bf16[8,8,768]{2,1,0:T(8,128)(2,1)S(1)} %all-to-all-done.got_ref, bf16[64,1440]{1,0:T(8,128)(2,1)S(1)} %get-tuple-element.15.padded_ref, f32[64,720]{1,0:T(8,128)S(1)} %get-tuple-element.16.outputs_ref), custom_call_target="tpu_custom_call" | custom-call | flops 132710400 | bytes 1048576 | tf_op jit(solution)/shard_map/summed/pallas_call | solution.py:31
  20.7 0.0 copy-done.1
  20.7 1.1 %hidden.1 = (f32[24,1440]{1,0:T(8,128)S(1)}, bf16[24,1440]{1,0:T(8,128)(2,1)S(1)}) custom-call(bf16[64,720]{1,0:T(8,128)(2,1)S(1)} %get-tuple-element.21.scaled_ref, bf16[720,1440]{1,0:T(8,128)(2,1)S(1)} %bitcast.10), custom_call_target="tpu_custom_call" | custom-call | flops 132710400 | bytes 1048576 | tf_op jit(solution)/shard_map/hidden/pallas_call | solution.py:31
  21.8 1.8 %collective-permute-start.1 = (bf16[24,1440]{1,0:T(8,128)(2,1)S(1)}, bf16[24,1440]{1,0:T(8,128)(2,1)S(1)}, u32[]{:S(2)}, u32[]{:S(2)}) collective-permute-start(bf16[24,1440]{1,0:T(8,128)(2,1)S(1)} %get-tuple-element.23), channel_id=1, source_target_pairs={{0,4},{4,0},{1,5},{5,1},{2,6},{6,2},{3,7},{7,3},{8,12},{12,8},{9,1... | collective-permute-start | bytes 207368 | tf_op jit(solution)/shard_map/ppermute | solution.py:211
  23.5 11.4 %all_to_all.10.recv_ref = f32[32,1,128]{2,1,0:T(1,128)S(1)} all-to-all(f32[32,1,128]{2,1,0:T(1,128)S(1)} %get-tuple-element.17), channel_id=1, replica_groups=mesh['rep'=4,'fsdp'=2,'exp'=4] {'rep','fsdp','exp'}, dimensions={0} | all-to-all | bytes 32768 | tf_op jit(solution)/shard_map/all_to_all | solution.py:202
  35.0 0.0 copy-done.5
  35.0 2.2 %final.1 = (bf16[720,1440]{1,0:T(8,128)(2,1)}, f32[4,128]{1,0:T(4,128)}) custom-call(f32[32,1,128]{2,1,0:T(1,128)S(1)} %all_to_all.10.recv_ref, f32[720,1440]{1,0:T(8,128)S(1)} %get-tuple-element.18.summed_ref, s32[4,128]{1,0:T(4,128)S(1)} %bitcast.15, f32[32,128]{1,0:T(8,128)S(1)} %get-tuple-element.19.taken_ref), custom_call_target="tpu_custom_call" | custom-call | flops 1036800 | bytes 1048576 | tf_op jit(solution)/shard_map/final/pallas_call | solution.py:31
  37.2 0.0 collective-permute-done.1
  37.2 0.7 %fusion = bf16[1,1,24,1440]{3,2,1,0:T(8,128)(2,1)} fusion(f32[24,1440]{1,0:T(8,128)S(1)} %get-tuple-element.22, bf16[24,1440]{1,0:T(8,128)(2,1)S(1)} %collective-permute-done.1), kind=kLoop, calls=%fused_computation.1 | loop fusion | flops 103680 | bytes 276480 | tf_op jit(solution)/shard_map/reshape | solution.py:212
Async XLA Ops:
  0.6 1.0 %copy-start.2 = (bf16[128,1440]{0,1:T(8,128)(2,1)S(1)}, bf16[128,1440]{0,1:T(8,128)(2,1)}, u32[]{:S(2)}) copy-start(bf16[128,1440]{0,1:T(8,128)(2,1)} %param.5) | copy-start | bytes 1105924
  1.6 0.7 %copy-start.4 = (s32[128,4]{0,1:T(4,128)S(1)}, s32[128,4]{0,1:T(4,128)}, u32[]{:S(2)}) copy-start(s32[128,4]{0,1:T(4,128)} %param.6) | copy-start | bytes 6148
  2.3 0.7 %copy-start.6 = (bf16[128,4]{0,1:T(4,128)(2,1)S(1)}, bf16[128,4]{0,1:T(4,128)(2,1)}, u32[]{:S(2)}) copy-start(bf16[128,4]{0,1:T(4,128)(2,1)} %param.7) | copy-start | bytes 3076
  4.0 15.7 %all-to-all-start = ((bf16[8,8,768]{2,1,0:T(8,128)(2,1)}), bf16[8,8,768]{2,1,0:T(8,128)(2,1)S(1)}, u32[]{:S(2)}, u32[]{:S(2)}) async-start(bf16[8,8,768]{2,1,0:T(8,128)(2,1)} %get-tuple-element.14), calls=%async_computation | async-start | bytes 196608 | tf_op jit(solution)/shard_map/all_to_all | solution.py:188
  11.3 5.0 %collective-permute-start = (bf16[24,1440]{1,0:T(8,128)(2,1)}, bf16[24,1440]{1,0:T(8,128)(2,1)S(1)}, u32[]{:S(2)}, u32[]{:S(2)}) collective-permute-start(bf16[24,1440]{1,0:T(8,128)(2,1)} %bitcast.12), channel_id=1, source_target_pairs={{0,4},{4,0},{1,5},{5,1},{2,6},{6,2},{3,7},{7,3},{8,12},{12,8},{9,1... | collective-permute-start | bytes 207368 | tf_op jit(solution)/shard_map/ppermute | solution.py:189
  16.3 1.6 %copy-start = (bf16[1,720,1440]{2,1,0:T(8,128)(2,1)S(1)}, bf16[1,720,1440]{2,1,0:T(8,128)(2,1)}, u32[]{:S(2)}) copy-start(bf16[1,720,1440]{2,1,0:T(8,128)(2,1)} %param.9) | copy-start | bytes 6220804
  17.9 0.9 %copy-start.3 = (bf16[1,1,24,1440]{3,2,1,0:T(8,128)(2,1)S(1)}, bf16[1,1,24,1440]{3,2,1,0:T(8,128)(2,1)}, u32[]{:S(2)}) copy-start(bf16[1,1,24,1440]{3,2,1,0:T(8,128)(2,1)} %param.8) | copy-start | bytes 207364
  18.8 1.9 %copy-start.1 = (bf16[1,720,1440]{2,1,0:T(8,128)(2,1)S(1)}, bf16[1,720,1440]{2,1,0:T(8,128)(2,1)}, u32[]{:S(2)}) copy-start(bf16[1,720,1440]{2,1,0:T(8,128)(2,1)} %param.9) | copy-start | bytes 6220804
  18.8 16.2 %copy-start.5 = (s32[128,4]{0,1:T(4,128)S(1)}, s32[128,4]{0,1:T(4,128)}, u32[]{:S(2)}) copy-start(s32[128,4]{0,1:T(4,128)} %param.6) | copy-start | bytes 6148
  21.8 15.4 %collective-permute-start.1 = (bf16[24,1440]{1,0:T(8,128)(2,1)S(1)}, bf16[24,1440]{1,0:T(8,128)(2,1)S(1)}, u32[]{:S(2)}, u32[]{:S(2)}) collective-permute-start(bf16[24,1440]{1,0:T(8,128)(2,1)S(1)} %get-tuple-element.23), channel_id=1, source_target_pairs={{0,4},{4,0},{1,5},{5,1},{2,6},{6,2},{3,7},{7,3},{8,12},{12,8},{9,1... | collective-permute-start | bytes 207368 | tf_op jit(solution)/shard_map/ppermute | solution.py:211

commit v2 on v1

--- a/solution.py
+++ b/solution.py
@@ -7,6 +7,7 @@
 from jax.experimental.pallas import tpu as pltpu
 from jax.sharding import PartitionSpec as P
 
+
 clip_level = 40.0
 f32 = jnp.float32
 bf16 = jnp.bfloat16
@@ -25,7 +26,7 @@
     return lax.dot_general(a, b, (dims, ((), ())), preferred_element_type=f32)
 
 
-def call(kernel, outs, flops, name, scratch=(), out_specs=None, in_specs=None):
+def call(kernel, outs, flops, scratch=(), out_specs=None, in_specs=None):
     def run(*args):
         specs = in_specs or [pl.BlockSpec(memory_space=VMEM)] * len(args)
         return pl.pallas_call(
@@ -34,15 +35,26 @@
             in_specs=specs,
             out_specs=out_specs or [pl.BlockSpec(memory_space=VMEM)] * len(outs),
             scratch_shapes=list(scratch),
-            compiler_params=pltpu.CompilerParams(vmem_limit_bytes=48 * 1024 * 1024),
+            compiler_params=pltpu.CompilerParams(vmem_limit_bytes=24 * 1024 * 1024),
             cost_estimate=pl.CostEstimate(flops=flops, bytes_accessed=1 << 20, transcendentals=0),
-            name=name,
         )(*args)
 
     return run
 
 
-def route_kernel(fsdp, room, ids_ref, probs_ref, tok_ref, send_ref, taken_ref):
+def route_kernel(
+    fsdp, room, ids_in, probs_in, tok_in, hidden_in, send_ref, taken_ref, hidden_ref, ids_ref, probs_ref, tok_ref, sems
+):
+    loads = [
+        pltpu.make_async_copy(src, dst, sems.at[i])
+        for i, (src, dst) in enumerate(
+            ((ids_in, ids_ref), (probs_in, probs_ref), (tok_in, tok_ref), (hidden_in, hidden_ref))
+        )
+    ]
+    for load in loads:
+        load.start()
+    loads[0].wait()
+    loads[1].wait()
     choices, tokens = ids_ref.shape
     slots = taken_ref.shape[0]
     part = tok_ref.shape[0] // fsdp
@@ -64,30 +76,59 @@
     lane = iota((slots, width - part), 1)
     tail = jnp.where(lane == 0, prob, 0.0).astype(bf16)
     picker = picker.astype(bf16)
+    loads[2].wait()
     for f in range(fsdp):
         rows = dot(picker, tok_ref[f * part : (f + 1) * part, :], ((1,), (1,))).astype(bf16)
         block = jnp.concatenate([rows, tail], axis=1)
         count = slots // room
         send_ref[f * count : (f + 1) * count] = block.reshape(count, room, width)
-
-
-def outputs_kernel(capacity, room, *refs):
-    hidden_refs, weight_ref, padded_ref, outputs_ref = refs[:-3], refs[-3], refs[-2], refs[-1]
-    fsdp = len(hidden_refs)
-    rows = padded_ref.shape[0] // fsdp
-    slot_count = hidden_refs[0].shape[0]
-    me = lax.axis_index("fsdp")
+    loads[3].wait()
+
+
+def spread_rows(capacity, room, hidden, rows):
+    slot_count = hidden.shape[0]
     to, at = iota((rows, slot_count), 0), iota((rows, slot_count), 1)
     source, order = to // room, to % room
     spread = jnp.where((order < capacity) & (at == source * capacity + order), 1.0, 0.0).astype(bf16)
-    for d, ref in enumerate(hidden_refs):
+    return dot(spread, hidden, ((1,), (0,))).astype(bf16)
+
+
+def own_kernel(capacity, room, hidden_ref, weight_in, padded_ref, outputs_ref, weight_ref, sems):
+    chunks = sems.shape[0]
+    size = weight_in.shape[0] // chunks
+    copies = []
+    for c in range(chunks):
+        part = slice(c * size, (c + 1) * size)
+        copy = pltpu.make_async_copy(weight_in.at[part, :], weight_ref.at[part, :], sems.at[c])
+        copy.start()
+        copies.append(copy)
+    padded = spread_rows(capacity, room, hidden_ref[...], padded_ref.shape[0])
+    padded_ref[...] = padded
+    for copy in copies:
+        copy.wait()
+    outputs_ref[...] = dot(padded, weight_ref[...], ((1,), (1,)))
+
+
+def others_kernel(capacity, room, *refs):
+    fsdp = (len(refs) - 5) + 1
+    own_padded, own_outputs, weight_ref = refs[:3]
+    hidden_refs = refs[3:-2]
+    padded_ref, outputs_ref = refs[-2:]
+    rows = own_padded.shape[0]
+    me = lax.axis_index("fsdp")
+    for d in range(fsdp):
         group = lax.rem(me + fsdp - d, fsdp)
         where = pl.ds(pl.multiple_of(group * rows, rows), rows)
-        padded_ref[where, :] = dot(spread, ref[...], ((1,), (0,))).astype(bf16)
-    outputs_ref[...] = dot(padded_ref[...], weight_ref[...], ((1,), (1,)))
-
-
-def summed_kernel(replicas, got_ref, padded_ref, outputs_ref, summed_ref, scaled_ref, pack_ref):
+        if d == 0:
+            padded_ref[where, :] = own_padded[...]
+            outputs_ref[where, :] = own_outputs[...]
+        else:
+            padded = spread_rows(capacity, room, hidden_refs[d - 1][...], rows)
+            padded_ref[where, :] = padded
+            outputs_ref[where, :] = dot(padded, weight_ref[...], ((1,), (1,)))
+
+
+def summed_kernel(replicas, got_ref, padded_ref, outputs_ref, scaled_ref, pack_ref):
     blocks, room, width = got_ref.shape
     total = blocks * room
     part = outputs_ref.shape[1]
@@ -96,9 +137,7 @@
     prob = got[:, part : part + 1].astype(f32)
     scaled = (prob * rows).astype(bf16)
     scaled_ref[...] = scaled
-    summed = dot(scaled, padded_ref[...], ((0,), (0,)))
-    summed_ref[...] = summed
-    peak = jnp.max(jnp.abs(summed))
+    peak = jnp.max(jnp.abs(dot(scaled, padded_ref[...], ((0,), (0,)))))
     score = jnp.sum(rows * outputs_ref[...], axis=1, keepdims=True)
     lane = iota((total, 128), 1)
     order = iota((total, 128), 0) % room
@@ -109,7 +148,7 @@
         pack_ref[r * blocks : (r + 1) * blocks, 0, :] = packed
 
 
-def hidden_kernel(capacity, room, scaled_ref, weight_ref, own_ref, *send_refs):
+def hidden_kernel(capacity, room, scaled_ref, weight_ref, turned_ref, own_ref, *send_refs):
     fsdp = len(send_refs) + 1
     total = scaled_ref.shape[0]
     rows = total // fsdp
@@ -122,11 +161,12 @@
         where = pl.ds(pl.multiple_of(group * rows, rows), rows)
         dense = dot(pick, scaled_ref[where, :], ((1,), (0,))).astype(bf16)
         ref[...] = dot(dense, weight_ref[...], ((1,), (0,))).astype(ref.dtype)
-
-
-def final_kernel(
-    experts, fsdp, room, recv_ref, summed_ref, ids_ref, taken_ref, weight_ref, route_ref, held, sems
-):
+    turned_ref[...] = scaled_ref[...].T
+
+
+def final_kernel(experts, fsdp, room, recv_ref, turned_ref, padded_ref, ids_ref, taken_ref, own_ref, *refs):
+    other_refs = refs[: fsdp - 1]
+    weight_ref, route_ref, hidden_ref, held, sems = refs[fsdp - 1 :]
     devices = recv_ref.shape[0]
     blocks = fsdp * experts
     replica, expert = lax.axis_index("rep"), lax.axis_index("exp")
@@ -135,11 +175,12 @@
     peak = jnp.max(jnp.where((lane == room) & (row % experts == expert), recv, 0.0))
     factor = jnp.minimum(1.0, clip_level / (jnp.full((1, 1), peak, f32) + 1e-06))
     chunks = sems.shape[0]
-    size = summed_ref.shape[0] // chunks
+    size = turned_ref.shape[0] // chunks
     copies = []
     for c in range(chunks):
         part = slice(c * size, (c + 1) * size)
-        held[part, :] = (summed_ref[part, :] * factor).astype(bf16)
+        summed = dot(turned_ref[part, :], padded_ref[...], ((1,), (0,)))
+        held[part, :] = (summed * factor).astype(bf16)
         copy = pltpu.make_async_copy(held.at[part, :], weight_ref.at[part, :], sems.at[c])
         copy.start()
         copies.append(copy)
@@ -156,6 +197,10 @@
     for k in range(ids_ref.shape[0]):
         hit = ids_ref[k : k + 1, :] == slot_expert
         route_ref[k : k + 1, :] = jnp.sum(jnp.where(hit, found, 0.0), axis=0, keepdims=True)
+    total = own_ref[...]
+    for ref in other_refs:
+        total = total + ref[...].astype(f32)
+    hidden_ref[...] = total.astype(bf16)
     for copy in copies:
         copy.wait()
 
@@ -179,48 +224,60 @@
     def ring(d):
         return [(i, (i + d) % fsdp) for i in range(fsdp)]
 
-    send, taken = call(
+    any_space, vmem = pl.BlockSpec(memory_space=pl.ANY), pl.BlockSpec(memory_space=VMEM)
+
+    def stay(x):
+        return pltpu.with_memory_space_constraint(x, pltpu.HBM)
+
+    sizes = [c for c in range(8, 161, 8) if part % c == 0] or [part]
+    chunks = part // sizes[-1]
+    send, taken, hidden = call(
         functools.partial(route_kernel, fsdp, room),
-        [shape((blocks, room, padded), bf16), shape((slots, tokens), f32)],
+        [shape((blocks, room, padded), bf16), shape((slots, tokens), f32), shape((slot_count, width), bf16)],
         2 * slots * tokens * features,
-        "route",
-    )(ids, route_probs.T, tok_grad.T)
+        in_specs=[any_space] * 4,
+        scratch=[
+            VMEM((choices, tokens), jnp.int32),
+            VMEM((choices, tokens), bf16),
+            VMEM((features, tokens), bf16),
+            pltpu.SemaphoreType.DMA((4,)),
+        ],
+    )(stay(ids), stay(route_probs.T), stay(tok_grad.T), stay(hidden))
     got = lax.all_to_all(send, ("fsdp", "exp"), split_axis=0, concat_axis=0, tiled=True)
-    hiddens = [hidden] + [lax.ppermute(hidden, "fsdp", ring(d)) for d in range(1, fsdp)]
+    others = [lax.ppermute(hidden_slots[0, 0], "fsdp", ring(d)) for d in range(1, fsdp)]
+    own_padded, own_outputs, weight = call(
+        functools.partial(own_kernel, capacity, room),
+        [shape((slots, width), bf16), shape((slots, part), f32), shape((part, width), bf16)],
+        2 * total * part * width,
+        in_specs=[vmem, any_space],
+        scratch=[pltpu.SemaphoreType.DMA((chunks,))],
+    )(hidden, stay(weight))
     hidden_padded, outputs = call(
-        functools.partial(outputs_kernel, capacity, room),
+        functools.partial(others_kernel, capacity, room),
         [shape((total, width), bf16), shape((total, part), f32)],
         2 * total * part * width,
-        "outputs",
-    )(*hiddens, weight)
-    summed, scaled, pack = call(
+    )(own_padded, own_outputs, weight, *others)
+    scaled, pack = call(
         functools.partial(summed_kernel, replicas),
-        [shape((part, width), f32), shape((total, part), bf16), shape((devices, 1, 128), f32)],
+        [shape((total, part), bf16), shape((devices, 1, 128), f32)],
         2 * total * part * width,
-        "summed",
     )(got, hidden_padded, outputs)
     recv = lax.all_to_all(pack, ("rep", "fsdp", "exp"), split_axis=0, concat_axis=0, tiled=True)
-    own, *others = call(
+    turned, own, *sends = call(
         functools.partial(hidden_kernel, capacity, room),
-        [shape((slot_count, width), f32)] + [shape((slot_count, width), bf16)] * (fsdp - 1),
+        [shape((part, total), bf16), shape((slot_count, width), f32)]
+        + [shape((slot_count, width), bf16)] * (fsdp - 1),
         2 * total * part * width,
-        "hidden",
     )(scaled, weight)
-    hidden_acc = own
-    for d in range(1, fsdp):
-        hidden_acc = hidden_acc + lax.ppermute(others[d - 1], "fsdp", ring(d)).astype(f32)
-    hidden_grad = hidden_acc.astype(bf16).reshape(1, 1, slot_count, width)
-    sizes = [c for c in range(16, 161, 16) if part % c == 0] or [part]
-    chunks = part // sizes[-1]
-    weight_grad, route_grad = call(
+    parts = [lax.ppermute(sends[d - 1], "fsdp", ring(d)) for d in range(1, fsdp)]
+    weight_grad, route_grad, hidden_grad = call(
         functools.partial(final_kernel, experts, fsdp, room),
-        [shape((part, width), bf16), shape((choices, tokens), f32)],
+        [shape((part, width), bf16), shape((choices, tokens), f32), shape((slot_count, width), bf16)],
         part * width,
-        "final",
         scratch=[VMEM((part, width), bf16), pltpu.SemaphoreType.DMA((chunks,))],
-        out_specs=[pl.BlockSpec(memory_space=pl.ANY), pl.BlockSpec(memory_space=VMEM)],
-    )(recv, summed, ids, taken)
-    return route_grad.T, hidden_grad, weight_grad.reshape(1, 1, part, width)
+        out_specs=[any_space, vmem, vmem],
+    )(recv, turned, hidden_padded, ids, taken, own, *parts)
+    return route_grad.T, hidden_grad[None, None], weight_grad.reshape(1, 1, part, width)
 
 
 def solution(mesh):
@@ -231,6 +288,7 @@
         P(("rep", "fsdp"), "exp", None, None),
         P("exp", "fsdp", None),
     )
+
     return jax.shard_map(
         on_device,
         mesh=mesh,

time: 38.2 us -> 33.6 us (0.88)
  local copies, waits for them, and re-layouts: 4.85 us -> 0.01 us
  Pallas kernels: 6.17 us -> 9.47 us
  starting transfers between devices: 11.1 us -> 9.94 us
  waiting for transfers between devices: 2.94 us -> 2.1 us
  other arithmetic: 0.65 us -> 0 us
    unnamed x14 -> x2, local copies, waits for them, and re-layouts: 4.85 us -> 0.01 us
    pallas_call x5 -> x6, Pallas kernels: 6.17 us -> 9.47 us  [run(): pl.pallas_call(kernel, out_shape=outs, in_specs=specs, out_specs=out_spec...]
    ppermute x2, waiting for transfers between devices: 2.93 us -> 0.58 us  [the longest x1 0.58 us: on_device(): lax.ppermute(hidden_slots[0, 0], 'fsdp', ring(d))]
    all_to_all x1, waiting for transfers between devices: 0.01 us -> 1.53 us  [on_device(): lax.all_to_all(send, ('fsdp', 'exp'), split_axis=0, concat_axis=0, tiled=...]
    ppermute x2, starting transfers between devices: 3.8 us -> 2.61 us  [the longest x1 2.02 us: on_device(): lax.ppermute(hidden_slots[0, 0], 'fsdp', ring(d))]
    reshape x1 -> x0, other arithmetic: 0.65 us -> none  [on_device(): hidden_grad = hidden_acc.astype(bf16).reshape(1, 1, slot_count, width)]
  transfers between devices with their start and end apart: 3 -> 3, of which waited for: 1 -> 2; matrix products, arithmetic and copies ran while one was open for 0% -> 0% of each run, Pallas kernels for 8% -> 9%
where the time goes in v2:
time: 33.6 us; the launch traced here: 33.3 us
  blocking collectives  11.1 us (33%)
  starting transfers between devices  9.94 us (30%)
  Pallas kernels  9.47 us (28%)
  waiting for transfers between devices  2.1 us (6%)
  between operations  0.66 us (2%)
    all_to_all x1, blocking collectives, on_device(): lax.all_to_all(pack, ('rep', 'fsdp', 'exp'), split_axis=0, concat_axis=0,...  11.1 us
    pallas_call x6, Pallas kernels, run(): pl.pallas_call(kernel, out_shape=outs, in_specs=specs, out_specs=out_spec...  9.47 us
    all_to_all x1, starting transfers between devices, on_device(): lax.all_to_all(send, ('fsdp', 'exp'), split_axis=0, concat_axis=0, tiled=...  7.32 us
    ppermute x1, starting transfers between devices, on_device(): lax.ppermute(hidden_slots[0, 0], 'fsdp', ring(d))  2.02 us
    all_to_all x1, waiting for transfers between devices, on_device(): lax.all_to_all(send, ('fsdp', 'exp'), split_axis=0, concat_axis=0, tiled=...  1.53 us
  transfers between devices with their start and end apart: 3, of which 2 were waited for; matrix products, arithmetic and copies ran while one was open for 0% of the time, Pallas kernels for 9%

profile of v2, /device:TPU:0, one launch (start us, length us, event | category | flops | bytes accessed | tf_op | source)
XLA Modules:
  0.0 33.3 jit_solution(4802291647250643038)
XLA Ops:
  0.6 2.0 %shard_map.76 = (bf16[8,8,768]{2,1,0:T(8,128)(2,1)}, f32[32,128]{1,0:T(8,128)S(1)}, bf16[24,1440]{1,0:T(8,128)(2,1)S(1)}) custom-call(s32[4,128]{1,0:T(4,128)} %bitcast.8, bf16[4,128]{1,0:T(4,128)(2,1)} %bitcast.14, bf16[1440,128]{1,0:T(8,128)(2,1)} %bitcast.11, bf16[24,1440]{1,0:T(8,128)(2,1)} %bitcast.12), custom_call_target="tpu_custom_call" | custom-call | flops 11796480 | bytes 1048576 | tf_op jit(solution)/shard_map/pallas_call | solution.py:32
  2.6 7.3 %all-to-all-start = ((bf16[8,8,768]{2,1,0:T(8,128)(2,1)}), bf16[8,8,768]{2,1,0:T(8,128)(2,1)S(1)}, u32[]{:S(2)}, u32[]{:S(2)}) async-start(bf16[8,8,768]{2,1,0:T(8,128)(2,1)} %get-tuple-element.19), calls=%async_computation | async-start | bytes 196608 | tf_op jit(solution)/shard_map/all_to_all | solution.py:246
  9.9 2.0 %collective-permute-start = (bf16[24,1440]{1,0:T(8,128)(2,1)}, bf16[24,1440]{1,0:T(8,128)(2,1)S(1)}, u32[]{:S(2)}, u32[]{:S(2)}) collective-permute-start(bf16[24,1440]{1,0:T(8,128)(2,1)} %bitcast.13), channel_id=1, source_target_pairs={{0,4},{4,0},{1,5},{5,1},{2,6},{6,2},{3,7},{7,3},{8,12},{12,8},{9,1... | collective-permute-start | bytes 207368 | tf_op jit(solution)/shard_map/ppermute | solution.py:247
  12.0 2.3 %shard_map.77 = (bf16[32,1440]{1,0:T(8,128)(2,1)S(1)}, f32[32,720]{1,0:T(8,128)S(1)}, bf16[720,1440]{1,0:T(8,128)(2,1)S(1)}) custom-call(bf16[24,1440]{1,0:T(8,128)(2,1)S(1)} %get-tuple-element.20.hidden_ref, bf16[720,1440]{1,0:T(8,128)(2,1)} %bitcast.10), custom_call_target="tpu_custom_call" | custom-call | flops 132710400 | bytes 1048576 | tf_op jit(solution)/shard_map/pallas_call | solution.py:32
  14.3 0.6 %collective-permute-done.refs_3_ = bf16[24,1440]{1,0:T(8,128)(2,1)S(1)} collective-permute-done((bf16[24,1440]{1,0:T(8,128)(2,1)}, bf16[24,1440]{1,0:T(8,128)(2,1)S(1)}, u32[]{:S(2)}, u32[]{:S(2)}) %collective-permute-start) | collective-permute-done | bytes 69152 | tf_op jit(solution)/shard_map/ppermute | solution.py:247
  14.9 0.0 copy-start
  14.9 0.8 %shard_map.78 = (bf16[64,1440]{1,0:T(8,128)(2,1)S(1)}, f32[64,720]{1,0:T(8,128)S(1)}) custom-call(bf16[32,1440]{1,0:T(8,128)(2,1)S(1)} %get-tuple-element.21.refs_0_, f32[32,720]{1,0:T(8,128)S(1)} %get-tuple-element.22.refs_1_, bf16[720,1440]{1,0:T(8,128)(2,1)S(1)} %get-tuple-element.23.refs_2_.weight_ref, bf16[24,1440]{1,0:T(8,128)(2,1)S(1)} %collective-permute-done.refs_3_), custom_call_target="tpu_custom_call" | custom-call | flops 132710400 | bytes 1048576 | tf_op jit(solution)/shard_map/pallas_call | solution.py:32
  15.7 1.5 %all-to-all-done.got_ref = bf16[8,8,768]{2,1,0:T(8,128)(2,1)S(1)} async-done(((bf16[8,8,768]{2,1,0:T(8,128)(2,1)}), bf16[8,8,768]{2,1,0:T(8,128)(2,1)S(1)}, u32[]{:S(2)}, u32[]{:S(2)}) %all-to-all-start) | async-done | bytes 98336 | tf_op jit(solution)/shard_map/all_to_all | solution.py:246
  17.2 1.0 %shard_map.79 = (bf16[64,720]{1,0:T(8,128)(2,1)S(1)}, f32[32,1,128]{2,1,0:T(1,128)S(1)}) custom-call(bf16[8,8,768]{2,1,0:T(8,128)(2,1)S(1)} %all-to-all-done.got_ref, bf16[64,1440]{1,0:T(8,128)(2,1)S(1)} %get-tuple-element.24.padded_ref, f32[64,720]{1,0:T(8,128)S(1)} %get-tuple-element.25.outputs_ref), custom_call_target="tpu_custom_call" | custom-call | flops 132710400 | bytes 1048576 | tf_op jit(solution)/shard_map/pallas_call | solution.py:32
  18.2 1.1 %shard_map.80 = (bf16[720,64]{1,0:T(8,128)(2,1)S(1)}, f32[24,1440]{1,0:T(8,128)S(1)}, bf16[24,1440]{1,0:T(8,128)(2,1)S(1)}) custom-call(bf16[64,720]{1,0:T(8,128)(2,1)S(1)} %get-tuple-element.27.scaled_ref, bf16[720,1440]{1,0:T(8,128)(2,1)S(1)} %get-tuple-element.23.refs_2_.weight_ref), custom_call_target="tpu_custom_call" | custom-call | flops 132710400 | bytes 1048576 | tf_op jit(solution)/shard_map/pallas_call | solution.py:32
  19.3 0.6 %collective-permute-start.1 = (bf16[24,1440]{1,0:T(8,128)(2,1)S(1)}, bf16[24,1440]{1,0:T(8,128)(2,1)S(1)}, u32[]{:S(2)}, u32[]{:S(2)}) collective-permute-start(bf16[24,1440]{1,0:T(8,128)(2,1)S(1)} %get-tuple-element.31), channel_id=1, source_target_pairs={{0,4},{4,0},{1,5},{5,1},{2,6},{6,2},{3,7},{7,3},{8,12},{12,8},{9,1... | collective-permute-start | bytes 207368 | tf_op jit(solution)/shard_map/ppermute | solution.py:272
  19.9 11.1 %all_to_all.10.recv_ref = f32[32,1,128]{2,1,0:T(1,128)S(1)} all-to-all(f32[32,1,128]{2,1,0:T(1,128)S(1)} %get-tuple-element.26), channel_id=1, replica_groups=mesh['rep'=4,'fsdp'=2,'exp'=4] {'rep','fsdp','exp'}, dimensions={0} | all-to-all | bytes 32768 | tf_op jit(solution)/shard_map/all_to_all | solution.py:265
  31.0 0.0 collective-permute-done.1.refs_0_
  31.0 0.0 copy-done
  31.0 2.3 %shard_map.81 = (bf16[720,1440]{1,0:T(8,128)(2,1)}, f32[4,128]{1,0:T(4,128)}, bf16[24,1440]{1,0:T(8,128)(2,1)}) custom-call(f32[32,1,128]{2,1,0:T(1,128)S(1)} %all_to_all.10.recv_ref, bf16[720,64]{1,0:T(8,128)(2,1)S(1)} %get-tuple-element.28.turned_ref, bf16[64,1440]{1,0:T(8,128)(2,1)S(1)} %get-tuple-element.24.padded_ref, s32[4,128]{1,0:T(4,128)S(1)} %bitcast.9, ...), custom_call_target="tpu_custom_call" | custom-call | flops 1036800 | bytes 1048576 | tf_op jit(solution)/shard_map/pallas_call | solution.py:32
Async XLA Ops:
  2.6 14.6 %all-to-all-start = ((bf16[8,8,768]{2,1,0:T(8,128)(2,1)}), bf16[8,8,768]{2,1,0:T(8,128)(2,1)S(1)}, u32[]{:S(2)}, u32[]{:S(2)}) async-start(bf16[8,8,768]{2,1,0:T(8,128)(2,1)} %get-tuple-element.19), calls=%async_computation | async-start | bytes 196608 | tf_op jit(solution)/shard_map/all_to_all | solution.py:246
  9.9 5.0 %collective-permute-start = (bf16[24,1440]{1,0:T(8,128)(2,1)}, bf16[24,1440]{1,0:T(8,128)(2,1)S(1)}, u32[]{:S(2)}, u32[]{:S(2)}) collective-permute-start(bf16[24,1440]{1,0:T(8,128)(2,1)} %bitcast.13), channel_id=1, source_target_pairs={{0,4},{4,0},{1,5},{5,1},{2,6},{6,2},{3,7},{7,3},{8,12},{12,8},{9,1... | collective-permute-start | bytes 207368 | tf_op jit(solution)/shard_map/ppermute | solution.py:247
  14.9 16.1 %copy-start = (s32[128,4]{0,1:T(4,128)S(1)}, s32[128,4]{0,1:T(4,128)}, u32[]{:S(2)}) copy-start(s32[128,4]{0,1:T(4,128)} %param.6) | copy-start | bytes 6148
  19.3 11.7 %collective-permute-start.1 = (bf16[24,1440]{1,0:T(8,128)(2,1)S(1)}, bf16[24,1440]{1,0:T(8,128)(2,1)S(1)}, u32[]{:S(2)}, u32[]{:S(2)}) collective-permute-start(bf16[24,1440]{1,0:T(8,128)(2,1)S(1)} %get-tuple-element.31), channel_id=1, source_target_pairs={{0,4},{4,0},{1,5},{5,1},{2,6},{6,2},{3,7},{7,3},{8,12},{12,8},{9,1... | collective-permute-start | bytes 207368 | tf_op jit(solution)/shard_map/ppermute | solution.py:272

commit v3 on v2

--- a/solution.py
+++ b/solution.py
@@ -43,12 +43,12 @@
 
 
 def route_kernel(
-    fsdp, room, ids_in, probs_in, tok_in, hidden_in, send_ref, taken_ref, hidden_ref, ids_ref, probs_ref, tok_ref, sems
+    fsdp, room, ids_in, probs_in, tok_in, send_ref, taken_ref, ids_ref, probs_ref, tok_ref, held, sems, out_sems
 ):
     loads = [
         pltpu.make_async_copy(src, dst, sems.at[i])
         for i, (src, dst) in enumerate(
-            ((ids_in, ids_ref), (probs_in, probs_ref), (tok_in, tok_ref), (hidden_in, hidden_ref))
+            ((ids_in, ids_ref), (probs_in, probs_ref), (tok_in, tok_ref))
         )
     ]
     for load in loads:
@@ -77,12 +77,18 @@
     tail = jnp.where(lane == 0, prob, 0.0).astype(bf16)
     picker = picker.astype(bf16)
     loads[2].wait()
+    stores = []
     for f in range(fsdp):
         rows = dot(picker, tok_ref[f * part : (f + 1) * part, :], ((1,), (1,))).astype(bf16)
         block = jnp.concatenate([rows, tail], axis=1)
         count = slots // room
-        send_ref[f * count : (f + 1) * count] = block.reshape(count, room, width)
-    loads[3].wait()
+        where = slice(f * count, (f + 1) * count)
+        held[where] = block.reshape(count, room, width)
+        store = pltpu.make_async_copy(held.at[where], send_ref.at[where], out_sems.at[f])
+        store.start()
+        stores.append(store)
+    for store in stores:
+        store.wait()
 
 
 def spread_rows(capacity, room, hidden, rows):
@@ -93,39 +99,31 @@
     return dot(spread, hidden, ((1,), (0,))).astype(bf16)
 
 
-def own_kernel(capacity, room, hidden_ref, weight_in, padded_ref, outputs_ref, weight_ref, sems):
+def outputs_kernel(capacity, room, fsdp, own_in, weight_in, *refs):
+    other_refs = refs[: fsdp - 1]
+    padded_ref, outputs_ref, weight_ref, own_ref, own_sem, sems = refs[fsdp - 1 :]
+    part = weight_in.shape[0]
+    rows = padded_ref.shape[0] // fsdp
     chunks = sems.shape[0]
-    size = weight_in.shape[0] // chunks
+    size = round_up(-(-part // chunks), 128)
+    own = pltpu.make_async_copy(own_in, own_ref, own_sem)
+    own.start()
     copies = []
     for c in range(chunks):
-        part = slice(c * size, (c + 1) * size)
-        copy = pltpu.make_async_copy(weight_in.at[part, :], weight_ref.at[part, :], sems.at[c])
+        where = slice(c * size, min((c + 1) * size, part))
+        copy = pltpu.make_async_copy(weight_in.at[where, :], weight_ref.at[where, :], sems.at[c])
         copy.start()
-        copies.append(copy)
-    padded = spread_rows(capacity, room, hidden_ref[...], padded_ref.shape[0])
-    padded_ref[...] = padded
-    for copy in copies:
+        copies.append((where, copy))
+    me = lax.axis_index("fsdp")
+    own.wait()
+    for d, ref in enumerate((own_ref,) + other_refs):
+        group = lax.rem(me + fsdp - d, fsdp)
+        to = pl.ds(pl.multiple_of(group * rows, rows), rows)
+        padded_ref[to, :] = spread_rows(capacity, room, ref[...], rows)
+    padded = padded_ref[...]
+    for where, copy in copies:
         copy.wait()
-    outputs_ref[...] = dot(padded, weight_ref[...], ((1,), (1,)))
-
-
-def others_kernel(capacity, room, *refs):
-    fsdp = (len(refs) - 5) + 1
-    own_padded, own_outputs, weight_ref = refs[:3]
-    hidden_refs = refs[3:-2]
-    padded_ref, outputs_ref = refs[-2:]
-    rows = own_padded.shape[0]
-    me = lax.axis_index("fsdp")
-    for d in range(fsdp):
-        group = lax.rem(me + fsdp - d, fsdp)
-        where = pl.ds(pl.multiple_of(group * rows, rows), rows)
-        if d == 0:
-            padded_ref[where, :] = own_padded[...]
-            outputs_ref[where, :] = own_outputs[...]
-        else:
-            padded = spread_rows(capacity, room, hidden_refs[d - 1][...], rows)
-            padded_ref[where, :] = padded
-            outputs_ref[where, :] = dot(padded, weight_ref[...], ((1,), (1,)))
+        outputs_ref[:, where] = dot(padded, weight_ref[where, :], ((1,), (1,)))
 
 
 def summed_kernel(replicas, got_ref, padded_ref, outputs_ref, scaled_ref, pack_ref):
@@ -166,7 +164,7 @@
 
 def final_kernel(experts, fsdp, room, recv_ref, turned_ref, padded_ref, ids_ref, taken_ref, own_ref, *refs):
     other_refs = refs[: fsdp - 1]
-    weight_ref, route_ref, hidden_ref, held, sems = refs[fsdp - 1 :]
+    weight_ref, route_out, hidden_out, held, route_ref, hidden_ref, sems, small_sems = refs[fsdp - 1 :]
     devices = recv_ref.shape[0]
     blocks = fsdp * experts
     replica, expert = lax.axis_index("rep"), lax.axis_index("exp")
@@ -197,10 +195,14 @@
     for k in range(ids_ref.shape[0]):
         hit = ids_ref[k : k + 1, :] == slot_expert
         route_ref[k : k + 1, :] = jnp.sum(jnp.where(hit, found, 0.0), axis=0, keepdims=True)
+    copies.append(pltpu.make_async_copy(route_ref, route_out, small_sems.at[0]))
+    copies[-1].start()
     total = own_ref[...]
     for ref in other_refs:
         total = total + ref[...].astype(f32)
     hidden_ref[...] = total.astype(bf16)
+    copies.append(pltpu.make_async_copy(hidden_ref, hidden_out, small_sems.at[1]))
+    copies[-1].start()
     for copy in copies:
         copy.wait()
 
@@ -231,32 +233,35 @@
 
     sizes = [c for c in range(8, 161, 8) if part % c == 0] or [part]
     chunks = part // sizes[-1]
-    send, taken, hidden = call(
+    send, taken = call(
         functools.partial(route_kernel, fsdp, room),
-        [shape((blocks, room, padded), bf16), shape((slots, tokens), f32), shape((slot_count, width), bf16)],
+        [pltpu.HBM((blocks, room, padded), bf16), shape((slots, tokens), f32)],
         2 * slots * tokens * features,
-        in_specs=[any_space] * 4,
+        in_specs=[any_space] * 3,
+        out_specs=[any_space, vmem],
         scratch=[
             VMEM((choices, tokens), jnp.int32),
             VMEM((choices, tokens), bf16),
             VMEM((features, tokens), bf16),
-            pltpu.SemaphoreType.DMA((4,)),
+            VMEM((blocks, room, padded), bf16),
+            pltpu.SemaphoreType.DMA((3,)),
+            pltpu.SemaphoreType.DMA((fsdp,)),
         ],
-    )(stay(ids), stay(route_probs.T), stay(tok_grad.T), stay(hidden))
+    )(stay(ids), stay(route_probs.T), stay(tok_grad.T))
     got = lax.all_to_all(send, ("fsdp", "exp"), split_axis=0, concat_axis=0, tiled=True)
-    others = [lax.ppermute(hidden_slots[0, 0], "fsdp", ring(d)) for d in range(1, fsdp)]
-    own_padded, own_outputs, weight = call(
-        functools.partial(own_kernel, capacity, room),
-        [shape((slots, width), bf16), shape((slots, part), f32), shape((part, width), bf16)],
+    others = [lax.ppermute(hidden, "fsdp", ring(d)) for d in range(1, fsdp)]
+    weight_chunks = -(-part // 256)
+    hidden_padded, outputs, weight = call(
+        functools.partial(outputs_kernel, capacity, room, fsdp),
+        [shape((total, width), bf16), shape((total, part), f32), shape((part, width), bf16)],
         2 * total * part * width,
-        in_specs=[vmem, any_space],
-        scratch=[pltpu.SemaphoreType.DMA((chunks,))],
-    )(hidden, stay(weight))
-    hidden_padded, outputs = call(
-        functools.partial(others_kernel, capacity, room),
-        [shape((total, width), bf16), shape((total, part), f32)],
-        2 * total * part * width,
-    )(own_padded, own_outputs, weight, *others)
+        in_specs=[any_space] * 2 + [vmem] * (fsdp - 1),
+        scratch=[
+            VMEM((slot_count, width), bf16),
+            pltpu.SemaphoreType.DMA,
+            pltpu.SemaphoreType.DMA((weight_chunks,)),
+        ],
+    )(stay(hidden), stay(weight), *others)
     scaled, pack = call(
         functools.partial(summed_kernel, replicas),
         [shape((total, part), bf16), shape((devices, 1, 128), f32)],
@@ -272,10 +277,20 @@
     parts = [lax.ppermute(sends[d - 1], "fsdp", ring(d)) for d in range(1, fsdp)]
     weight_grad, route_grad, hidden_grad = call(
         functools.partial(final_kernel, experts, fsdp, room),
-        [shape((part, width), bf16), shape((choices, tokens), f32), shape((slot_count, width), bf16)],
+        [
+            pltpu.HBM((part, width), bf16),
+            pltpu.HBM((choices, tokens), f32),
+            pltpu.HBM((slot_count, width), bf16),
+        ],
         part * width,
-        scratch=[VMEM((part, width), bf16), pltpu.SemaphoreType.DMA((chunks,))],
-        out_specs=[any_space, vmem, vmem],
+        scratch=[
+            VMEM((part, width), bf16),
+            VMEM((choices, tokens), f32),
+            VMEM((slot_count, width), bf16),
+            pltpu.SemaphoreType.DMA((chunks,)),
+            pltpu.SemaphoreType.DMA((2,)),
+        ],
+        out_specs=[any_space] * 3,
     )(recv, turned, hidden_padded, ids, taken, own, *parts)
     return route_grad.T, hidden_grad[None, None], weight_grad.reshape(1, 1, part, width)
 

time: 33.6 us -> 35.3 us (1.051)
  starting transfers between devices: 9.94 us -> 11.1 us
  waiting for transfers between devices: 2.1 us -> 2.94 us
  Pallas kernels: 9.47 us -> 8.84 us
    ppermute x1, waiting for transfers between devices: 0.58 us -> 2.93 us  [on_device(): others = [lax.ppermute(hidden, 'fsdp', ring(d)) for d in range(1, fsdp)]]
    all_to_all x1, waiting for transfers between devices: 1.53 us -> 0.01 us  [on_device(): lax.all_to_all(send, ('fsdp', 'exp'), split_axis=0, concat_axis=0, tiled=...]
    ppermute x1, starting transfers between devices: 0.59 us -> 1.79 us  [on_device(): lax.ppermute(sends[d - 1], 'fsdp', ring(d))]
    pallas_call x6 -> x5, Pallas kernels: 9.47 us -> 8.84 us  [run(): pl.pallas_call(kernel, out_shape=outs, in_specs=specs, out_specs=out_spec...]
  transfers between devices with their start and end apart: 3 -> 3, of which waited for: 2 -> 1; matrix products, arithmetic and copies ran while one was open for 0% -> 0% of each run, Pallas kernels for 9% -> 9%
where the time goes in v3:
time: 35.3 us; the launch traced here: 35 us
  blocking collectives  11.4 us (32%)
  starting transfers between devices  11.1 us (31%)
  Pallas kernels  8.84 us (25%)
  waiting for transfers between devices  2.94 us (8%)
  between operations  0.67 us (2%)
    all_to_all x1, blocking collectives, on_device(): lax.all_to_all(pack, ('rep', 'fsdp', 'exp'), split_axis=0, concat_axis=0,...  11.4 us
    pallas_call x5, Pallas kernels, run(): pl.pallas_call(kernel, out_shape=outs, in_specs=specs, out_specs=out_spec...  8.84 us
    all_to_all x1, starting transfers between devices, on_device(): lax.all_to_all(send, ('fsdp', 'exp'), split_axis=0, concat_axis=0, tiled=...  7.32 us
    ppermute x1, waiting for transfers between devices, on_device(): others = [lax.ppermute(hidden, 'fsdp', ring(d)) for d in range(1, fsdp)]  2.93 us
    ppermute x1, starting transfers between devices, on_device(): others = [lax.ppermute(hidden, 'fsdp', ring(d)) for d in range(1, fsdp)]  2.02 us
    ppermute x1, starting transfers between devices, on_device(): lax.ppermute(sends[d - 1], 'fsdp', ring(d))  1.79 us
  transfers between devices with their start and end apart: 3, of which 1 were waited for; matrix products, arithmetic and copies ran while one was open for 0% of the time, Pallas kernels for 9%

profile of v3, /device:TPU:0, one launch (start us, length us, event | category | flops | bytes accessed | tf_op | source)
XLA Modules:
  0.0 35.0 jit_solution(10353766009776355515)
XLA Ops:
  0.6 2.0 %shard_map.76 = (bf16[8,8,768]{2,1,0:T(8,128)(2,1)}, f32[32,128]{1,0:T(8,128)S(1)}) custom-call(s32[4,128]{1,0:T(4,128)} %bitcast.8, bf16[4,128]{1,0:T(4,128)(2,1)} %bitcast.14, bf16[1440,128]{1,0:T(8,128)(2,1)} %bitcast.11), custom_call_target="tpu_custom_call" | custom-call | flops 11796480 | bytes 1048576 | tf_op jit(solution)/shard_map/pallas_call | solution.py:32
  2.6 7.3 %all-to-all-start = ((bf16[8,8,768]{2,1,0:T(8,128)(2,1)}), bf16[8,8,768]{2,1,0:T(8,128)(2,1)S(1)}, u32[]{:S(2)}, u32[]{:S(2)}) async-start(bf16[8,8,768]{2,1,0:T(8,128)(2,1)} %get-tuple-element.16), calls=%async_computation | async-start | bytes 196608 | tf_op jit(solution)/shard_map/all_to_all | solution.py:251
  9.9 2.0 %collective-permute-start = (bf16[24,1440]{1,0:T(8,128)(2,1)}, bf16[24,1440]{1,0:T(8,128)(2,1)S(1)}, u32[]{:S(2)}, u32[]{:S(2)}) collective-permute-start(bf16[24,1440]{1,0:T(8,128)(2,1)} %bitcast.12), channel_id=1, source_target_pairs={{0,4},{4,0},{1,5},{5,1},{2,6},{6,2},{3,7},{7,3},{8,12},{12,8},{9,1... | collective-permute-start | bytes 207368 | tf_op jit(solution)/shard_map/ppermute | solution.py:252
  11.9 2.9 %collective-permute-done.refs_0_ = bf16[24,1440]{1,0:T(8,128)(2,1)S(1)} collective-permute-done((bf16[24,1440]{1,0:T(8,128)(2,1)}, bf16[24,1440]{1,0:T(8,128)(2,1)S(1)}, u32[]{:S(2)}, u32[]{:S(2)}) %collective-permute-start) | collective-permute-done | bytes 69152 | tf_op jit(solution)/shard_map/ppermute | solution.py:252
  14.9 0.0 copy-start
  14.9 3.1 %shard_map.77 = (bf16[64,1440]{1,0:T(8,128)(2,1)S(1)}, f32[64,720]{1,0:T(8,128)S(1)}, bf16[720,1440]{1,0:T(8,128)(2,1)S(1)}) custom-call(bf16[24,1440]{1,0:T(8,128)(2,1)} %bitcast.13, bf16[720,1440]{1,0:T(8,128)(2,1)} %bitcast.10, bf16[24,1440]{1,0:T(8,128)(2,1)S(1)} %collective-permute-done.refs_0_), custom_call_target="tpu_custom_call" | custom-call | flops 132710400 | bytes 1048576 | tf_op jit(solution)/shard_map/pallas_call | solution.py:32
  17.9 0.0 all-to-all-done.got_ref
  18.0 1.0 %shard_map.78 = (bf16[64,720]{1,0:T(8,128)(2,1)S(1)}, f32[32,1,128]{2,1,0:T(1,128)S(1)}) custom-call(bf16[8,8,768]{2,1,0:T(8,128)(2,1)S(1)} %all-to-all-done.got_ref, bf16[64,1440]{1,0:T(8,128)(2,1)S(1)} %get-tuple-element.17.padded_ref, f32[64,720]{1,0:T(8,128)S(1)} %get-tuple-element.18.outputs_ref), custom_call_target="tpu_custom_call" | custom-call | flops 132710400 | bytes 1048576 | tf_op jit(solution)/shard_map/pallas_call | solution.py:32
  19.0 1.1 %shard_map.79 = (bf16[720,64]{1,0:T(8,128)(2,1)S(1)}, f32[24,1440]{1,0:T(8,128)S(1)}, bf16[24,1440]{1,0:T(8,128)(2,1)S(1)}) custom-call(bf16[64,720]{1,0:T(8,128)(2,1)S(1)} %get-tuple-element.20.scaled_ref, bf16[720,1440]{1,0:T(8,128)(2,1)S(1)} %get-tuple-element.21.weight_ref), custom_call_target="tpu_custom_call" | custom-call | flops 132710400 | bytes 1048576 | tf_op jit(solution)/shard_map/pallas_call | solution.py:32
  20.1 1.8 %collective-permute-start.1 = (bf16[24,1440]{1,0:T(8,128)(2,1)S(1)}, bf16[24,1440]{1,0:T(8,128)(2,1)S(1)}, u32[]{:S(2)}, u32[]{:S(2)}) collective-permute-start(bf16[24,1440]{1,0:T(8,128)(2,1)S(1)} %get-tuple-element.25), channel_id=1, source_target_pairs={{0,4},{4,0},{1,5},{5,1},{2,6},{6,2},{3,7},{7,3},{8,12},{12,8},{9,1... | collective-permute-start | bytes 207368 | tf_op jit(solution)/shard_map/ppermute | solution.py:277
  21.9 11.4 %all_to_all.10.recv_ref = f32[32,1,128]{2,1,0:T(1,128)S(1)} all-to-all(f32[32,1,128]{2,1,0:T(1,128)S(1)} %get-tuple-element.19), channel_id=1, replica_groups=mesh['rep'=4,'fsdp'=2,'exp'=4] {'rep','fsdp','exp'}, dimensions={0} | all-to-all | bytes 32768 | tf_op jit(solution)/shard_map/all_to_all | solution.py:270
  33.3 0.0 collective-permute-done.1.refs_0_
  33.3 0.0 copy-done
  33.3 1.7 %shard_map.80 = (bf16[720,1440]{1,0:T(8,128)(2,1)}, f32[4,128]{1,0:T(4,128)}, bf16[24,1440]{1,0:T(8,128)(2,1)}) custom-call(f32[32,1,128]{2,1,0:T(1,128)S(1)} %all_to_all.10.recv_ref, bf16[720,64]{1,0:T(8,128)(2,1)S(1)} %get-tuple-element.22.turned_ref, bf16[64,1440]{1,0:T(8,128)(2,1)S(1)} %get-tuple-element.17.padded_ref, s32[4,128]{1,0:T(4,128)S(1)} %bitcast.9, ...), custom_call_target="tpu_custom_call" | custom-call | flops 1036800 | bytes 1048576 | tf_op jit(solution)/shard_map/pallas_call | solution.py:32
Async XLA Ops:
  2.6 15.4 %all-to-all-start = ((bf16[8,8,768]{2,1,0:T(8,128)(2,1)}), bf16[8,8,768]{2,1,0:T(8,128)(2,1)S(1)}, u32[]{:S(2)}, u32[]{:S(2)}) async-start(bf16[8,8,768]{2,1,0:T(8,128)(2,1)} %get-tuple-element.16), calls=%async_computation | async-start | bytes 196608 | tf_op jit(solution)/shard_map/all_to_all | solution.py:251
  9.9 5.0 %collective-permute-start = (bf16[24,1440]{1,0:T(8,128)(2,1)}, bf16[24,1440]{1,0:T(8,128)(2,1)S(1)}, u32[]{:S(2)}, u32[]{:S(2)}) collective-permute-start(bf16[24,1440]{1,0:T(8,128)(2,1)} %bitcast.12), channel_id=1, source_target_pairs={{0,4},{4,0},{1,5},{5,1},{2,6},{6,2},{3,7},{7,3},{8,12},{12,8},{9,1... | collective-permute-start | bytes 207368 | tf_op jit(solution)/shard_map/ppermute | solution.py:252
  14.9 18.4 %copy-start = (s32[128,4]{0,1:T(4,128)S(1)}, s32[128,4]{0,1:T(4,128)}, u32[]{:S(2)}) copy-start(s32[128,4]{0,1:T(4,128)} %param.6) | copy-start | bytes 6148
  20.1 13.2 %collective-permute-start.1 = (bf16[24,1440]{1,0:T(8,128)(2,1)S(1)}, bf16[24,1440]{1,0:T(8,128)(2,1)S(1)}, u32[]{:S(2)}, u32[]{:S(2)}) collective-permute-start(bf16[24,1440]{1,0:T(8,128)(2,1)S(1)} %get-tuple-element.25), channel_id=1, source_target_pairs={{0,4},{4,0},{1,5},{5,1},{2,6},{6,2},{3,7},{7,3},{8,12},{12,8},{9,1... | collective-permute-start | bytes 207368 | tf_op jit(solution)/shard_map/ppermute | solution.py:277

commit v4 on v3

--- a/solution.py
+++ b/solution.py
@@ -43,7 +43,7 @@
 
 
 def route_kernel(
-    fsdp, room, ids_in, probs_in, tok_in, send_ref, taken_ref, ids_ref, probs_ref, tok_ref, held, sems, out_sems
+    fsdp, room, lead, ids_in, probs_in, tok_in, send_ref, taken_ref, ids_ref, probs_ref, tok_ref, held, sems, out_sems
 ):
     loads = [
         pltpu.make_async_copy(src, dst, sems.at[i])
@@ -84,6 +84,9 @@
         count = slots // room
         where = slice(f * count, (f + 1) * count)
         held[where] = block.reshape(count, room, width)
+        if f == 0 and lead > 0:
+            held[0] = block[lead * room : (lead + 1) * room]
+            held[lead] = block[:room]
         store = pltpu.make_async_copy(held.at[where], send_ref.at[where], out_sems.at[f])
         store.start()
         stores.append(store)
@@ -123,14 +126,17 @@
     padded = padded_ref[...]
     for where, copy in copies:
         copy.wait()
-        outputs_ref[:, where] = dot(padded, weight_ref[where, :], ((1,), (1,)))
-
-
-def summed_kernel(replicas, got_ref, padded_ref, outputs_ref, scaled_ref, pack_ref):
+    outputs_ref[...] = dot(padded, weight_ref[...], ((1,), (1,)))
+
+
+def summed_kernel(replicas, lead, got_ref, padded_ref, outputs_ref, scaled_ref, pack_ref):
     blocks, room, width = got_ref.shape
     total = blocks * room
     part = outputs_ref.shape[1]
     got = got_ref[...].reshape(total, width)
+    if lead > 0:
+        near, far = got[:room], got[lead * room : (lead + 1) * room]
+        got = jnp.concatenate([far, got[room : lead * room], near, got[(lead + 1) * room :]], axis=0) if lead > 1 else jnp.concatenate([far, near, got[2 * room :]], axis=0)
     rows = got[:, :part].astype(f32)
     prob = got[:, part : part + 1].astype(f32)
     scaled = (prob * rows).astype(bf16)
@@ -199,7 +205,7 @@
     copies[-1].start()
     total = own_ref[...]
     for ref in other_refs:
-        total = total + ref[...].astype(f32)
+        total = total + ref[...]
     hidden_ref[...] = total.astype(bf16)
     copies.append(pltpu.make_async_copy(hidden_ref, hidden_out, small_sems.at[1]))
     copies[-1].start()
@@ -222,6 +228,9 @@
     shape = jax.ShapeDtypeStruct
     hidden, weight = hidden_slots[0, 0], down_weight[0]
     ids = expert_ids.T
+    lead = (experts - 1) // 2
+    order = list(range(blocks))
+    order[0], order[lead] = lead, 0
 
     def ring(d):
         return [(i, (i + d) % fsdp) for i in range(fsdp)]
@@ -234,7 +243,7 @@
     sizes = [c for c in range(8, 161, 8) if part % c == 0] or [part]
     chunks = part // sizes[-1]
     send, taken = call(
-        functools.partial(route_kernel, fsdp, room),
+        functools.partial(route_kernel, fsdp, room, lead),
         [pltpu.HBM((blocks, room, padded), bf16), shape((slots, tokens), f32)],
         2 * slots * tokens * features,
         in_specs=[any_space] * 3,
@@ -248,7 +257,14 @@
             pltpu.SemaphoreType.DMA((fsdp,)),
         ],
     )(stay(ids), stay(route_probs.T), stay(tok_grad.T))
-    got = lax.all_to_all(send, ("fsdp", "exp"), split_axis=0, concat_axis=0, tiled=True)
+    got = lax.all_to_all(
+        send,
+        ("fsdp", "exp"),
+        split_axis=0,
+        concat_axis=0,
+        axis_index_groups=[order],
+        tiled=True,
+    )
     others = [lax.ppermute(hidden, "fsdp", ring(d)) for d in range(1, fsdp)]
     weight_chunks = -(-part // 256)
     hidden_padded, outputs, weight = call(
@@ -263,15 +279,14 @@
         ],
     )(stay(hidden), stay(weight), *others)
     scaled, pack = call(
-        functools.partial(summed_kernel, replicas),
+        functools.partial(summed_kernel, replicas, lead),
         [shape((total, part), bf16), shape((devices, 1, 128), f32)],
         2 * total * part * width,
     )(got, hidden_padded, outputs)
     recv = lax.all_to_all(pack, ("rep", "fsdp", "exp"), split_axis=0, concat_axis=0, tiled=True)
     turned, own, *sends = call(
         functools.partial(hidden_kernel, capacity, room),
-        [shape((part, total), bf16), shape((slot_count, width), f32)]
-        + [shape((slot_count, width), bf16)] * (fsdp - 1),
+        [shape((part, total), bf16)] + [shape((slot_count, width), f32)] * fsdp,
         2 * total * part * width,
     )(scaled, weight)
     parts = [lax.ppermute(sends[d - 1], "fsdp", ring(d)) for d in range(1, fsdp)]

time: 35.3 us -> 33.8 us (0.958)
  blocking collectives: 11.4 us -> 10.6 us
  Pallas kernels: 8.84 us -> 8.15 us
  waiting for transfers between devices: 2.94 us -> 3.37 us
  starting transfers between devices: 11.1 us -> 10.7 us
    all_to_all x1, blocking collectives: 11.4 us -> 10.6 us  [on_device(): lax.all_to_all(pack, ('rep', 'fsdp', 'exp'), split_axis=0, concat_axis=0,...]
    pallas_call x5, Pallas kernels: 8.84 us -> 8.15 us  [run(): pl.pallas_call(kernel, out_shape=outs, in_specs=specs, out_specs=out_spec...]
    all_to_all x1, starting transfers between devices: 7.32 us -> 7.88 us  [on_device(): lax.all_to_all(send, ('fsdp', 'exp'), split_axis=0, concat_axis=0, axis_i...]
    ppermute x1, starting transfers between devices: 2.02 us -> 1.46 us  [on_device(): others = [lax.ppermute(hidden, 'fsdp', ring(d)) for d in range(1, fsdp)]]
    ppermute x1, starting transfers between devices: 1.79 us -> 1.35 us  [on_device(): lax.ppermute(sends[d - 1], 'fsdp', ring(d))]
    ppermute x1, waiting for transfers between devices: 2.93 us -> 3.36 us  [on_device(): others = [lax.ppermute(hidden, 'fsdp', ring(d)) for d in range(1, fsdp)]]
  transfers between devices with their start and end apart: 3 -> 3, of which waited for: 1 -> 1; matrix products, arithmetic and copies ran while one was open for 0% -> 0% of each run, Pallas kernels for 9% -> 7%
where the time goes in v4:
time: 33.8 us; the launch traced here: 33.5 us
  starting transfers between devices  10.7 us (32%)
  blocking collectives  10.6 us (31%)
  Pallas kernels  8.15 us (24%)
  waiting for transfers between devices  3.37 us (10%)
  between operations  0.67 us (2%)
    all_to_all x1, blocking collectives, on_device(): lax.all_to_all(pack, ('rep', 'fsdp', 'exp'), split_axis=0, concat_axis=0,...  10.6 us
    pallas_call x5, Pallas kernels, run(): pl.pallas_call(kernel, out_shape=outs, in_specs=specs, out_specs=out_spec...  8.15 us
    all_to_all x1, starting transfers between devices, on_device(): lax.all_to_all(send, ('fsdp', 'exp'), split_axis=0, concat_axis=0, axis_i...  7.88 us
    ppermute x1, waiting for transfers between devices, on_device(): others = [lax.ppermute(hidden, 'fsdp', ring(d)) for d in range(1, fsdp)]  3.36 us
    ppermute x1, starting transfers between devices, on_device(): others = [lax.ppermute(hidden, 'fsdp', ring(d)) for d in range(1, fsdp)]  1.46 us
    ppermute x1, starting transfers between devices, on_device(): lax.ppermute(sends[d - 1], 'fsdp', ring(d))  1.35 us
  transfers between devices with their start and end apart: 3, of which 1 were waited for; matrix products, arithmetic and copies ran while one was open for 0% of the time, Pallas kernels for 7%

profile of v4, /device:TPU:0, one launch (start us, length us, event | category | flops | bytes accessed | tf_op | source)
XLA Modules:
  0.0 33.5 jit_solution(8946465551649165096)
XLA Ops:
  0.6 2.0 %shard_map.76 = (bf16[8,8,768]{2,1,0:T(8,128)(2,1)}, f32[32,128]{1,0:T(8,128)S(1)}) custom-call(s32[4,128]{1,0:T(4,128)} %bitcast.8, bf16[4,128]{1,0:T(4,128)(2,1)} %bitcast.14, bf16[1440,128]{1,0:T(8,128)(2,1)} %bitcast.11), custom_call_target="tpu_custom_call" | custom-call | flops 11796480 | bytes 1048576 | tf_op jit(solution)/shard_map/pallas_call | solution.py:32
  2.6 7.9 %all-to-all-start = ((bf16[8,8,768]{2,1,0:T(8,128)(2,1)}), bf16[8,8,768]{2,1,0:T(8,128)(2,1)S(1)}, u32[]{:S(2)}, u32[]{:S(2)}) async-start(bf16[8,8,768]{2,1,0:T(8,128)(2,1)} %get-tuple-element.16), calls=%async_computation | async-start | bytes 196608 | tf_op jit(solution)/shard_map/all_to_all | solution.py:260
  10.5 1.5 %collective-permute-start = (bf16[24,1440]{1,0:T(8,128)(2,1)}, bf16[24,1440]{1,0:T(8,128)(2,1)S(1)}, u32[]{:S(2)}, u32[]{:S(2)}) collective-permute-start(bf16[24,1440]{1,0:T(8,128)(2,1)} %bitcast.12), channel_id=1, source_target_pairs={{0,4},{4,0},{1,5},{5,1},{2,6},{6,2},{3,7},{7,3},{8,12},{12,8},{9,1... | collective-permute-start | bytes 207368 | tf_op jit(solution)/shard_map/ppermute | solution.py:268
  11.9 3.4 %collective-permute-done.refs_0_ = bf16[24,1440]{1,0:T(8,128)(2,1)S(1)} collective-permute-done((bf16[24,1440]{1,0:T(8,128)(2,1)}, bf16[24,1440]{1,0:T(8,128)(2,1)S(1)}, u32[]{:S(2)}, u32[]{:S(2)}) %collective-permute-start) | collective-permute-done | bytes 69152 | tf_op jit(solution)/shard_map/ppermute | solution.py:268
  15.3 0.0 copy-start
  15.3 2.4 %shard_map.77 = (bf16[64,1440]{1,0:T(8,128)(2,1)S(1)}, f32[64,720]{1,0:T(8,128)S(1)}, bf16[720,1440]{1,0:T(8,128)(2,1)S(1)}) custom-call(bf16[24,1440]{1,0:T(8,128)(2,1)} %bitcast.13, bf16[720,1440]{1,0:T(8,128)(2,1)} %bitcast.10, bf16[24,1440]{1,0:T(8,128)(2,1)S(1)} %collective-permute-done.refs_0_), custom_call_target="tpu_custom_call" | custom-call | flops 132710400 | bytes 1048576 | tf_op jit(solution)/shard_map/pallas_call | solution.py:32
  17.8 0.0 all-to-all-done.got_ref
  17.8 1.0 %shard_map.78 = (bf16[64,720]{1,0:T(8,128)(2,1)S(1)}, f32[32,1,128]{2,1,0:T(1,128)S(1)}) custom-call(bf16[8,8,768]{2,1,0:T(8,128)(2,1)S(1)} %all-to-all-done.got_ref, bf16[64,1440]{1,0:T(8,128)(2,1)S(1)} %get-tuple-element.17.padded_ref, f32[64,720]{1,0:T(8,128)S(1)} %get-tuple-element.18.outputs_ref), custom_call_target="tpu_custom_call" | custom-call | flops 132710400 | bytes 1048576 | tf_op jit(solution)/shard_map/pallas_call | solution.py:32
  18.8 1.1 %shard_map.79 = (bf16[720,64]{1,0:T(8,128)(2,1)S(1)}, f32[24,1440]{1,0:T(8,128)S(1)}, f32[24,1440]{1,0:T(8,128)S(1)}) custom-call(bf16[64,720]{1,0:T(8,128)(2,1)S(1)} %get-tuple-element.20.scaled_ref, bf16[720,1440]{1,0:T(8,128)(2,1)S(1)} %get-tuple-element.21.weight_ref), custom_call_target="tpu_custom_call" | custom-call | flops 132710400 | bytes 1048576 | tf_op jit(solution)/shard_map/pallas_call | solution.py:32
  19.8 1.4 %collective-permute-start.1 = (f32[24,1440]{1,0:T(8,128)S(1)}, f32[24,1440]{1,0:T(8,128)S(1)}, u32[]{:S(2)}, u32[]{:S(2)}) collective-permute-start(f32[24,1440]{1,0:T(8,128)S(1)} %get-tuple-element.25), channel_id=1, source_target_pairs={{0,4},{4,0},{1,5},{5,1},{2,6},{6,2},{3,7},{7,3},{8,12},{12,8},{9,1... | collective-permute-start | bytes 414728 | tf_op jit(solution)/shard_map/ppermute | solution.py:292
  21.2 10.6 %all_to_all.10.recv_ref = f32[32,1,128]{2,1,0:T(1,128)S(1)} all-to-all(f32[32,1,128]{2,1,0:T(1,128)S(1)} %get-tuple-element.19), channel_id=1, replica_groups=mesh['rep'=4,'fsdp'=2,'exp'=4] {'rep','fsdp','exp'}, dimensions={0} | all-to-all | bytes 32768 | tf_op jit(solution)/shard_map/all_to_all | solution.py:286
  31.8 0.0 collective-permute-done.1.refs_0_
  31.8 0.0 copy-done
  31.8 1.7 %shard_map.80 = (bf16[720,1440]{1,0:T(8,128)(2,1)}, f32[4,128]{1,0:T(4,128)}, bf16[24,1440]{1,0:T(8,128)(2,1)}) custom-call(f32[32,1,128]{2,1,0:T(1,128)S(1)} %all_to_all.10.recv_ref, bf16[720,64]{1,0:T(8,128)(2,1)S(1)} %get-tuple-element.22.turned_ref, bf16[64,1440]{1,0:T(8,128)(2,1)S(1)} %get-tuple-element.17.padded_ref, s32[4,128]{1,0:T(4,128)S(1)} %bitcast.9, ...), custom_call_target="tpu_custom_call" | custom-call | flops 1036800 | bytes 1048576 | tf_op jit(solution)/shard_map/pallas_call | solution.py:32
Async XLA Ops:
  2.6 15.2 %all-to-all-start = ((bf16[8,8,768]{2,1,0:T(8,128)(2,1)}), bf16[8,8,768]{2,1,0:T(8,128)(2,1)S(1)}, u32[]{:S(2)}, u32[]{:S(2)}) async-start(bf16[8,8,768]{2,1,0:T(8,128)(2,1)} %get-tuple-element.16), calls=%async_computation | async-start | bytes 196608 | tf_op jit(solution)/shard_map/all_to_all | solution.py:260
  10.5 4.8 %collective-permute-start = (bf16[24,1440]{1,0:T(8,128)(2,1)}, bf16[24,1440]{1,0:T(8,128)(2,1)S(1)}, u32[]{:S(2)}, u32[]{:S(2)}) collective-permute-start(bf16[24,1440]{1,0:T(8,128)(2,1)} %bitcast.12), channel_id=1, source_target_pairs={{0,4},{4,0},{1,5},{5,1},{2,6},{6,2},{3,7},{7,3},{8,12},{12,8},{9,1... | collective-permute-start | bytes 207368 | tf_op jit(solution)/shard_map/ppermute | solution.py:268
  15.3 16.5 %copy-start = (s32[128,4]{0,1:T(4,128)S(1)}, s32[128,4]{0,1:T(4,128)}, u32[]{:S(2)}) copy-start(s32[128,4]{0,1:T(4,128)} %param.6) | copy-start | bytes 6148
  19.8 11.9 %collective-permute-start.1 = (f32[24,1440]{1,0:T(8,128)S(1)}, f32[24,1440]{1,0:T(8,128)S(1)}, u32[]{:S(2)}, u32[]{:S(2)}) collective-permute-start(f32[24,1440]{1,0:T(8,128)S(1)} %get-tuple-element.25), channel_id=1, source_target_pairs={{0,4},{4,0},{1,5},{5,1},{2,6},{6,2},{3,7},{7,3},{8,12},{12,8},{9,1... | collective-permute-start | bytes 414728 | tf_op jit(solution)/shard_map/ppermute | solution.py:292

commit v5 on v4

--- a/solution.py
+++ b/solution.py
@@ -129,7 +129,7 @@
     outputs_ref[...] = dot(padded, weight_ref[...], ((1,), (1,)))
 
 
-def summed_kernel(replicas, lead, got_ref, padded_ref, outputs_ref, scaled_ref, pack_ref):
+def summed_kernel(replicas, lead, got_ref, padded_ref, outputs_ref, scaled_ref, pack_out, pack_ref, sem):
     blocks, room, width = got_ref.shape
     total = blocks * room
     part = outputs_ref.shape[1]
@@ -150,21 +150,30 @@
     packed = jnp.where(iota((blocks, 128), 1) == room, peak, packed)
     for r in range(replicas):
         pack_ref[r * blocks : (r + 1) * blocks, 0, :] = packed
-
-
-def hidden_kernel(capacity, room, scaled_ref, weight_ref, turned_ref, own_ref, *send_refs):
-    fsdp = len(send_refs) + 1
-    total = scaled_ref.shape[0]
-    rows = total // fsdp
-    slot_count = own_ref.shape[0]
-    me = lax.axis_index("fsdp")
+    store = pltpu.make_async_copy(pack_ref, pack_out, sem)
+    store.start()
+    store.wait()
+
+
+def partial_grad(capacity, room, shift, rows, slot_count, scaled_ref, weight_ref):
+    fsdp = scaled_ref.shape[0] // rows
+    group = lax.rem(lax.axis_index("fsdp") + shift, fsdp)
     to, at = iota((slot_count, rows), 0), iota((slot_count, rows), 1)
     pick = jnp.where(at == to // capacity * room + to % capacity, 1.0, 0.0).astype(bf16)
-    for d, ref in enumerate((own_ref,) + send_refs):
-        group = lax.rem(me + d, fsdp)
-        where = pl.ds(pl.multiple_of(group * rows, rows), rows)
-        dense = dot(pick, scaled_ref[where, :], ((1,), (0,))).astype(bf16)
-        ref[...] = dot(dense, weight_ref[...], ((1,), (0,))).astype(ref.dtype)
+    where = pl.ds(pl.multiple_of(group * rows, rows), rows)
+    dense = dot(pick, scaled_ref[where, :], ((1,), (0,))).astype(bf16)
+    return dot(dense, weight_ref[...], ((1,), (0,)))
+
+
+def sends_kernel(capacity, room, scaled_ref, weight_ref, *send_refs):
+    rows = scaled_ref.shape[0] // (len(send_refs) + 1)
+    for d, ref in enumerate(send_refs):
+        ref[...] = partial_grad(capacity, room, d + 1, rows, ref.shape[0], scaled_ref, weight_ref)
+
+
+def keep_kernel(capacity, room, fsdp, scaled_ref, weight_ref, turned_ref, own_ref):
+    rows = scaled_ref.shape[0] // fsdp
+    own_ref[...] = partial_grad(capacity, room, 0, rows, own_ref.shape[0], scaled_ref, weight_ref)
     turned_ref[...] = scaled_ref[...].T
 
 
@@ -240,7 +249,7 @@
     def stay(x):
         return pltpu.with_memory_space_constraint(x, pltpu.HBM)
 
-    sizes = [c for c in range(8, 161, 8) if part % c == 0] or [part]
+    sizes = [c for c in range(8, 81, 8) if part % c == 0] or [part]
     chunks = part // sizes[-1]
     send, taken = call(
         functools.partial(route_kernel, fsdp, room, lead),
@@ -280,16 +289,23 @@
     )(stay(hidden), stay(weight), *others)
     scaled, pack = call(
         functools.partial(summed_kernel, replicas, lead),
-        [shape((total, part), bf16), shape((devices, 1, 128), f32)],
+        [shape((total, part), bf16), pltpu.HBM((devices, 1, 128), f32)],
         2 * total * part * width,
+        out_specs=[vmem, any_space],
+        scratch=[VMEM((devices, 1, 128), f32), pltpu.SemaphoreType.DMA],
     )(got, hidden_padded, outputs)
     recv = lax.all_to_all(pack, ("rep", "fsdp", "exp"), split_axis=0, concat_axis=0, tiled=True)
-    turned, own, *sends = call(
-        functools.partial(hidden_kernel, capacity, room),
-        [shape((part, total), bf16)] + [shape((slot_count, width), f32)] * fsdp,
-        2 * total * part * width,
+    sends = call(
+        functools.partial(sends_kernel, capacity, room),
+        [shape((slot_count, width), f32)] * (fsdp - 1),
+        2 * slots * part * width,
     )(scaled, weight)
     parts = [lax.ppermute(sends[d - 1], "fsdp", ring(d)) for d in range(1, fsdp)]
+    turned, own = call(
+        functools.partial(keep_kernel, capacity, room, fsdp),
+        [shape((part, total), bf16), shape((slot_count, width), f32)],
+        2 * slots * part * width,
+    )(scaled, weight)
     weight_grad, route_grad, hidden_grad = call(
         functools.partial(final_kernel, experts, fsdp, room),
         [

time: 33.8 us -> 34 us (level)
  blocking collectives: 10.6 us -> 0 us
  waiting for transfers between devices: 3.37 us -> 9.84 us
  starting transfers between devices: 10.7 us -> 14.3 us
  Pallas kernels: 8.15 us -> 8.84 us
    all_to_all x1 -> x0, blocking collectives: 10.6 us -> none  [on_device(): lax.all_to_all(pack, ('rep', 'fsdp', 'exp'), split_axis=0, concat_axis=0,...]
    all_to_all x0 -> x1, waiting for transfers between devices: none -> 6.47 us  [on_device(): lax.all_to_all(pack, ('rep', 'fsdp', 'exp'), split_axis=0, concat_axis=0,...]
    all_to_all x0 -> x1, starting transfers between devices: none -> 3.65 us  [on_device(): lax.all_to_all(pack, ('rep', 'fsdp', 'exp'), split_axis=0, concat_axis=0,...]
    pallas_call x5 -> x6, Pallas kernels: 8.15 us -> 8.84 us  [run(): pl.pallas_call(kernel, out_shape=outs, in_specs=specs, out_specs=out_spec...]
  transfers between devices with their start and end apart: 3 -> 4, of which waited for: 1 -> 2; matrix products, arithmetic and copies ran while one was open for 0% -> 0% of each run, Pallas kernels for 7% -> 9%
where the time goes in v5:
time: 34 us; the launch traced here: 33.7 us
  starting transfers between devices  14.3 us (42%)
  waiting for transfers between devices  9.84 us (29%)
  Pallas kernels  8.84 us (26%)
  between operations  0.68 us (2%)
    pallas_call x6, Pallas kernels, run(): pl.pallas_call(kernel, out_shape=outs, in_specs=specs, out_specs=out_spec...  8.84 us
    all_to_all x1, starting transfers between devices, on_device(): lax.all_to_all(send, ('fsdp', 'exp'), split_axis=0, concat_axis=0, axis_i...  7.88 us
    all_to_all x1, waiting for transfers between devices, on_device(): lax.all_to_all(pack, ('rep', 'fsdp', 'exp'), split_axis=0, concat_axis=0,...  6.47 us
    all_to_all x1, starting transfers between devices, on_device(): lax.all_to_all(pack, ('rep', 'fsdp', 'exp'), split_axis=0, concat_axis=0,...  3.65 us
    ppermute x1, waiting for transfers between devices, on_device(): others = [lax.ppermute(hidden, 'fsdp', ring(d)) for d in range(1, fsdp)]  3.36 us
    ppermute x1, starting transfers between devices, on_device(): others = [lax.ppermute(hidden, 'fsdp', ring(d)) for d in range(1, fsdp)]  1.46 us
    ppermute x1, starting transfers between devices, on_device(): lax.ppermute(sends[d - 1], 'fsdp', ring(d))  1.34 us
  transfers between devices with their start and end apart: 4, of which 2 were waited for; matrix products, arithmetic and copies ran while one was open for 0% of the time, Pallas kernels for 9%

profile of v5, /device:TPU:0, one launch (start us, length us, event | category | flops | bytes accessed | tf_op | source)
XLA Modules:
  0.0 33.7 jit_solution(14910707325171016029)
XLA Ops:
  0.6 2.0 %shard_map.76 = (bf16[8,8,768]{2,1,0:T(8,128)(2,1)}, f32[32,128]{1,0:T(8,128)S(1)}) custom-call(s32[4,128]{1,0:T(4,128)} %bitcast.8, bf16[4,128]{1,0:T(4,128)(2,1)} %bitcast.14, bf16[1440,128]{1,0:T(8,128)(2,1)} %bitcast.11), custom_call_target="tpu_custom_call" | custom-call | flops 11796480 | bytes 1048576 | tf_op jit(solution)/shard_map/pallas_call | solution.py:32
  2.6 7.9 %all-to-all-start = ((bf16[8,8,768]{2,1,0:T(8,128)(2,1)}), bf16[8,8,768]{2,1,0:T(8,128)(2,1)S(1)}, u32[]{:S(2)}, u32[]{:S(2)}) async-start(bf16[8,8,768]{2,1,0:T(8,128)(2,1)} %get-tuple-element.15), calls=%async_computation | async-start | bytes 196608 | tf_op jit(solution)/shard_map/all_to_all | solution.py:269
  10.5 1.5 %collective-permute-start = (bf16[24,1440]{1,0:T(8,128)(2,1)}, bf16[24,1440]{1,0:T(8,128)(2,1)S(1)}, u32[]{:S(2)}, u32[]{:S(2)}) collective-permute-start(bf16[24,1440]{1,0:T(8,128)(2,1)} %bitcast.12), channel_id=1, source_target_pairs={{0,4},{4,0},{1,5},{5,1},{2,6},{6,2},{3,7},{7,3},{8,12},{12,8},{9,1... | collective-permute-start | bytes 207368 | tf_op jit(solution)/shard_map/ppermute | solution.py:277
  11.9 3.4 %collective-permute-done.refs_0_ = bf16[24,1440]{1,0:T(8,128)(2,1)S(1)} collective-permute-done((bf16[24,1440]{1,0:T(8,128)(2,1)}, bf16[24,1440]{1,0:T(8,128)(2,1)S(1)}, u32[]{:S(2)}, u32[]{:S(2)}) %collective-permute-start) | collective-permute-done | bytes 69152 | tf_op jit(solution)/shard_map/ppermute | solution.py:277
  15.3 2.4 %shard_map.77 = (bf16[64,1440]{1,0:T(8,128)(2,1)S(1)}, f32[64,720]{1,0:T(8,128)S(1)}, bf16[720,1440]{1,0:T(8,128)(2,1)S(1)}) custom-call(bf16[24,1440]{1,0:T(8,128)(2,1)} %bitcast.13, bf16[720,1440]{1,0:T(8,128)(2,1)} %bitcast.10, bf16[24,1440]{1,0:T(8,128)(2,1)S(1)} %collective-permute-done.refs_0_), custom_call_target="tpu_custom_call" | custom-call | flops 132710400 | bytes 1048576 | tf_op jit(solution)/shard_map/pallas_call | solution.py:32
  17.7 0.0 all-to-all-done.got_ref
  17.8 1.6 %shard_map.78 = (bf16[64,720]{1,0:T(8,128)(2,1)S(1)}, f32[32,1,128]{2,1,0:T(1,128)}) custom-call(bf16[8,8,768]{2,1,0:T(8,128)(2,1)S(1)} %all-to-all-done.got_ref, bf16[64,1440]{1,0:T(8,128)(2,1)S(1)} %get-tuple-element.16.padded_ref, f32[64,720]{1,0:T(8,128)S(1)} %get-tuple-element.17.outputs_ref), custom_call_target="tpu_custom_call" | custom-call | flops 132710400 | bytes 1048576 | tf_op jit(solution)/shard_map/pallas_call | solution.py:32
  19.3 0.0 copy-start
  19.4 0.6 %shard_map.80 = f32[24,1440]{1,0:T(8,128)S(1)} custom-call(bf16[64,720]{1,0:T(8,128)(2,1)S(1)} %get-tuple-element.19.scaled_ref, bf16[720,1440]{1,0:T(8,128)(2,1)S(1)} %get-tuple-element.20.weight_ref), custom_call_target="tpu_custom_call" | custom-call | flops 66355200 | bytes 1048576 | tf_op jit(solution)/shard_map/pallas_call | solution.py:32
  19.9 1.3 %collective-permute-start.1 = (f32[24,1440]{1,0:T(8,128)S(1)}, f32[24,1440]{1,0:T(8,128)S(1)}, u32[]{:S(2)}, u32[]{:S(2)}) collective-permute-start(f32[24,1440]{1,0:T(8,128)S(1)} %shard_map.80), channel_id=1, source_target_pairs={{0,4},{4,0},{1,5},{5,1},{2,6},{6,2},{3,7},{7,3},{8,12},{12,8},{9,1... | collective-permute-start | bytes 414728 | tf_op jit(solution)/shard_map/ppermute | solution.py:303
  21.3 3.7 %all-to-all-start.1 = ((f32[32,1,128]{2,1,0:T(1,128)}), f32[32,1,128]{2,1,0:T(1,128)S(1)}, u32[]{:S(2)}, u32[]{:S(2)}) async-start(f32[32,1,128]{2,1,0:T(1,128)} %get-tuple-element.18), calls=%async_computation.1 | async-start | bytes 32768 | tf_op jit(solution)/shard_map/all_to_all | solution.py:297
  25.0 0.6 %shard_map.79 = (bf16[720,64]{1,0:T(8,128)(2,1)S(1)}, f32[24,1440]{1,0:T(8,128)S(1)}) custom-call(bf16[64,720]{1,0:T(8,128)(2,1)S(1)} %get-tuple-element.19.scaled_ref, bf16[720,1440]{1,0:T(8,128)(2,1)S(1)} %get-tuple-element.20.weight_ref), custom_call_target="tpu_custom_call" | custom-call | flops 66355200 | bytes 1048576 | tf_op jit(solution)/shard_map/pallas_call | solution.py:32
  25.5 6.5 %all-to-all-done.1.recv_ref = f32[32,1,128]{2,1,0:T(1,128)S(1)} async-done(((f32[32,1,128]{2,1,0:T(1,128)}), f32[32,1,128]{2,1,0:T(1,128)S(1)}, u32[]{:S(2)}, u32[]{:S(2)}) %all-to-all-start.1) | async-done | bytes 16416 | tf_op jit(solution)/shard_map/all_to_all | solution.py:297
  32.0 0.0 collective-permute-done.1.refs_0_
  32.0 0.0 copy-done
  32.0 1.7 %shard_map.81 = (bf16[720,1440]{1,0:T(8,128)(2,1)}, f32[4,128]{1,0:T(4,128)}, bf16[24,1440]{1,0:T(8,128)(2,1)}) custom-call(f32[32,1,128]{2,1,0:T(1,128)S(1)} %all-to-all-done.1.recv_ref, bf16[720,64]{1,0:T(8,128)(2,1)S(1)} %get-tuple-element.21.turned_ref, bf16[64,1440]{1,0:T(8,128)(2,1)S(1)} %get-tuple-element.16.padded_ref, s32[4,128]{1,0:T(4,128)S(1)} %bitcast.9, ...), custom_call_target="tpu_custom_call" | custom-call | flops 1036800 | bytes 1048576 | tf_op jit(solution)/shard_map/pallas_call | solution.py:32
Async XLA Ops:
  2.6 15.2 %all-to-all-start = ((bf16[8,8,768]{2,1,0:T(8,128)(2,1)}), bf16[8,8,768]{2,1,0:T(8,128)(2,1)S(1)}, u32[]{:S(2)}, u32[]{:S(2)}) async-start(bf16[8,8,768]{2,1,0:T(8,128)(2,1)} %get-tuple-element.15), calls=%async_computation | async-start | bytes 196608 | tf_op jit(solution)/shard_map/all_to_all | solution.py:269
  10.5 4.8 %collective-permute-start = (bf16[24,1440]{1,0:T(8,128)(2,1)}, bf16[24,1440]{1,0:T(8,128)(2,1)S(1)}, u32[]{:S(2)}, u32[]{:S(2)}) collective-permute-start(bf16[24,1440]{1,0:T(8,128)(2,1)} %bitcast.12), channel_id=1, source_target_pairs={{0,4},{4,0},{1,5},{5,1},{2,6},{6,2},{3,7},{7,3},{8,12},{12,8},{9,1... | collective-permute-start | bytes 207368 | tf_op jit(solution)/shard_map/ppermute | solution.py:277
  19.3 12.7 %copy-start = (s32[128,4]{0,1:T(4,128)S(1)}, s32[128,4]{0,1:T(4,128)}, u32[]{:S(2)}) copy-start(s32[128,4]{0,1:T(4,128)} %param.6) | copy-start | bytes 6148
  19.9 12.1 %collective-permute-start.1 = (f32[24,1440]{1,0:T(8,128)S(1)}, f32[24,1440]{1,0:T(8,128)S(1)}, u32[]{:S(2)}, u32[]{:S(2)}) collective-permute-start(f32[24,1440]{1,0:T(8,128)S(1)} %shard_map.80), channel_id=1, source_target_pairs={{0,4},{4,0},{1,5},{5,1},{2,6},{6,2},{3,7},{7,3},{8,12},{12,8},{9,1... | collective-permute-start | bytes 414728 | tf_op jit(solution)/shard_map/ppermute | solution.py:303
  21.3 10.7 %all-to-all-start.1 = ((f32[32,1,128]{2,1,0:T(1,128)}), f32[32,1,128]{2,1,0:T(1,128)S(1)}, u32[]{:S(2)}, u32[]{:S(2)}) async-start(f32[32,1,128]{2,1,0:T(1,128)} %get-tuple-element.18), calls=%async_computation.1 | async-start | bytes 32768 | tf_op jit(solution)/shard_map/all_to_all | solution.py:297
